TPU v7x, 128 devices: a whole 4x4x4 slice. The times are simulated.
128 devices in a mesh: rep: 2 (over core), dp: 64 (over x, y, z).
Axes of the slice: x: 4, y: 4, z: 4, core: 2. Of those that a mesh axis runs over, the one named last changes fastest.
Arguments:
- g_w_gate: bfloat16 [128, 2, 640, 3200], P(('rep', 'dp')), parts along dimension 0
- g_w_up: bfloat16 [128, 2, 640, 3200], P(('rep', 'dp')), parts along dimension 0
- g_w_down: bfloat16 [128, 2, 3200, 640], P(('rep', 'dp')), parts along dimension 0
- w_gate: bfloat16 [2, 640, 3200], replicated
- w_up: bfloat16 [2, 640, 3200], replicated
- w_down: bfloat16 [2, 3200, 640], replicated
- m_w_gate: float32 [2, 640, 3200], P(None, 'dp')
- m_w_up: float32 [2, 640, 3200], P(None, 'dp')
- m_w_down: float32 [2, 3200, 640], P(None, 'dp')
- v_w_gate: float32 [2, 640, 3200], P(None, 'dp')
- v_w_up: float32 [2, 640, 3200], P(None, 'dp')
- v_w_down: float32 [2, 3200, 640], P(None, 'dp')
Outputs:
- output 1: bfloat16 [4, 640, 3200], P('rep'), parts along dimension 0
- output 2: bfloat16 [4, 640, 3200], P('rep'), parts along dimension 0
- output 3: bfloat16 [4, 3200, 640], P('rep'), parts along dimension 0
- output 4: float32 [4, 640, 3200], P('rep', 'dp'), parts along dimension 0
- output 5: float32 [4, 640, 3200], P('rep', 'dp'), parts along dimension 0
- output 6: float32 [4, 3200, 640], P('rep', 'dp'), parts along dimension 0
- output 7: float32 [4, 640, 3200], P('rep', 'dp'), parts along dimension 0
- output 8: float32 [4, 640, 3200], P('rep', 'dp'), parts along dimension 0
- output 9: float32 [4, 3200, 640], P('rep', 'dp'), parts along dimension 0
There are 2 independent parts. A program takes and returns all parts, laid end to end along the dimension named above; an argument that names none is the same for every part.
All inputs are finite; a program needn't handle non-finite values.
Results may differ from a plain program's by a relative error of at most 0.022.
Values are sent between devices in bfloat16 or wider.
A program may use at most 1.5 GiB of HBM per device.

v0:
```python
import jax
import jax.numpy as jnp
from jax import lax
from jax.sharding import PartitionSpec as P


def adamw(w, m, v, g):
    m = 0.9 * m + 0.1 * g
    v = 0.95 * v + 0.05 * g * g
    step = m * lax.rsqrt(v + 1e-8) + 0.1 * w
    return (w - 0.02 * step).astype(jnp.bfloat16), m, v


def clipped(gradients, sum_of_squares, count):
    factor = jnp.minimum(1.0, 0.5 * lax.rsqrt(sum_of_squares / count + 1e-30))
    return [g * factor for g in gradients]


def solution(mesh):
    def step(*arrays):
        terms, weights, m, v = (arrays[i : i + 3] for i in (0, 3, 6, 9))
        gradients = [lax.psum_scatter(t[0], "dp", scatter_dimension=1, tiled=True).astype(jnp.float32) for t in terms]
        squares = lax.psum(sum(jnp.sum(g * g) for g in gradients), "dp")
        gradients = clipped(gradients, squares, lax.psum(1, "dp") * sum(g.size for g in gradients))
        me = lax.axis_index("dp")
        own = [lax.dynamic_slice_in_dim(w, me * one.shape[1], one.shape[1], 1).astype(jnp.float32) for w, one in zip(weights, m, strict=True)]
        new = [adamw(w, m, v, g) for w, m, v, g in zip(own, m, v, gradients, strict=True)]
        whole = [lax.all_gather(one[0], "dp", axis=1, tiled=True) for one in new]
        return (*whole, *(one[1] for one in new), *(one[2] for one in new))

    all_of, cut = P(None, None, None), P(None, "dp", None)
    return jax.shard_map(
        step,
        mesh=mesh,
        in_specs=(P(("rep", "dp"), None, None, None),) * 3 + (all_of,) * 3 + (cut,) * 6,
        out_specs=(P("rep", None, None),) * 3 + (P("rep", "dp", None),) * 6,
        check_vma=False,
    )
```

profile of v0, /device:TPU:0, one launch (start us, length us, event | category | flops | bytes accessed | tf_op | source)
XLA Modules:
  0.0 791.3 jit_solution(6680888886062393495)
XLA Ops:
  7.2 0.0 all-reduce.6.cloned.1.call-start
  7.2 38.5 %copy.48 = bf16[1,2,3200,640]{3,1,2,0:T(2,128)(2,1)} copy(bf16[1,2,3200,640]{3,2,1,0:T(8,128)(2,1)} %param.14) | data formatting | bytes 16384000 | tf_op args[2]
  45.8 22.5 %copy.49 = bf16[1,2,640,3200]{3,1,2,0:T(2,128)(2,1)} copy(bf16[1,2,640,3200]{3,2,1,0:T(8,128)(2,1)S(1)} %copy-done) | data formatting | bytes 16384000 | tf_op args[1]
  68.3 22.5 %copy.50 = bf16[1,2,640,3200]{3,1,2,0:T(2,128)(2,1)} copy(bf16[1,2,640,3200]{3,2,1,0:T(8,128)(2,1)S(1)} %bitcast.14) | data formatting | bytes 16384000 | tf_op args[0]
  90.9 0.0 all-gather.6.cloned.1.call-start
  91.0 0.5 copy-done.7
  91.5 0.6 dynamic-slice
  93.4 265.9 %all-reduce.6.cloned.1.call-done = (bf16[2,640,3200]{2,0,1:T(2,128)(2,1)}, bf16[2,640,3200]{2,0,1:T(2,128)(2,1)}, bf16[2,3200,640]{2,0,1:T(2,128)(2,1)}) async-done(((bf16[2,640,3200]{2,0,1:T(2,128)(2,1)}, bf16[2,640,3200]{2,0,1:T(2,128)(2,1)}, bf16[2,3200,640]{2,0,1:T(2,128)(2,1)}), (bf16[2,640,3200]{2,0,1:T(2,128)(2,1)}, bf16[2,640,3200]{2,0,1:T(2,128)(2,1)}, ...) | async-done | bytes 24576016
  359.3 1.8 fusion.8
  362.5 1.8 fusion.10
  364.9 1.2 constant_dynamic-slice_fusion.1
  366.1 176.7 %psum.7 = f32[]{:T(128)} all-reduce(f32[]{:T(128)S(6)} %add.65), channel_id=1, replica_groups=mesh['rep'=2,'dp'=64] {'dp'}, use_global_device_ids=true, to_apply=%region_6.0 | all-reduce | flops 1 | bytes 8 | tf_op jit(solution)/shard_map/psum | solution.py:23
  543.5 2.4 fusion.19
  546.0 0.0 all-gather.4.cloned.1.call-start
  546.0 2.4 fusion.18
  548.4 0.2 all-gather.8.cloned.1.call-start
  548.7 1.0 constant_dynamic-slice_fusion
  549.6 2.4 fusion.20
  552.0 64.8 %all-gather.6.cloned.1.call-done = bf16[2,640,3200]{2,0,1:T(2,128)(2,1)} async-done(((bf16[2,10,3200]{2,0,1:T(2,128)(2,1)}), bf16[2,640,3200]{2,0,1:T(2,128)(2,1)}) %all-gather.6.cloned.1.call-update) | async-done | bytes 8192016 | tf_op jit(solution)/shard_map/all_gather | solution.py:28
  616.9 7.6 copy.37
  624.5 72.9 %all-gather.4.cloned.1.call-done = bf16[2,640,3200]{2,0,1:T(2,128)(2,1)} async-done(((bf16[2,10,3200]{2,0,1:T(2,128)(2,1)}), bf16[2,640,3200]{2,0,1:T(2,128)(2,1)}) %all-gather.4.cloned.1.call-update) | async-done | bytes 8192016 | tf_op jit(solution)/shard_map/all_gather | solution.py:28
  697.4 7.6 copy.36
  705.0 72.1 %all-gather.8.cloned.1.call-done = bf16[2,3200,640]{2,0,1:T(2,128)(2,1)} async-done(((bf16[2,50,640]{2,0,1:T(2,128)(2,1)}), bf16[2,3200,640]{2,0,1:T(2,128)(2,1)}) %all-gather.8.cloned.1.call-update) | async-done | bytes 8192016 | tf_op jit(solution)/shard_map/all_gather | solution.py:28
  777.1 7.7 copy.38
  (24 shorter events, 0.1 us)
Async XLA Ops:
  7.2 352.2 %all-reduce.6.cloned.1.call-start = ((), (), s32[]{:S(2)}) async-start(), calls=%async_computation.3 | async-start | bytes 49152000
  7.2 38.5 %copy-start = (bf16[1,2,640,3200]{3,2,1,0:T(8,128)(2,1)S(1)}, bf16[1,2,640,3200]{3,2,1,0:T(8,128)(2,1)}, u32[]{:S(2)}) copy-start(bf16[1,2,640,3200]{3,2,1,0:T(8,128)(2,1)} %param.13) | copy-start | bytes 24576004
  7.2 61.1 %slice-start = ((s8[8192000]{0:T(1024)(128)(4,1)}), s8[4194304]{0:T(1024)(128)(4,1)S(1)}, s32[]{:S(2)}) async-start(s8[8192000]{0:T(1024)(128)(4,1)} %bitcast.13), calls=%async_computation.4 | async-start | bytes 8388608
  45.8 22.6 %slice-start.1 = ((s8[8192000]{0:T(1024)(128)(4,1)}), s8[3997696]{0:T(1024)(128)(4,1)S(1)}, s32[]{:S(2)}) async-start(s8[8192000]{0:T(1024)(128)(4,1)} %bitcast.13), calls=%async_computation.5 | async-start | bytes 7995392
  90.9 0.7 copy-start.7
  90.9 452.6 %copy-start.1 = (f32[2,10,3200]{2,0,1:T(2,128)S(1)}, f32[2,10,3200]{2,0,1:T(2,128)}, u32[]{:S(2)}) copy-start(f32[2,10,3200]{2,0,1:T(2,128)} %param.22) | copy-start | bytes 768004
  90.9 452.6 %copy-start.2 = (f32[2,10,3200]{2,0,1:T(2,128)S(1)}, f32[2,10,3200]{2,0,1:T(2,128)}, u32[]{:S(2)}) copy-start(f32[2,10,3200]{2,0,1:T(2,128)} %param.19) | copy-start | bytes 768004
  90.9 455.1 %copy-start.3 = (f32[2,10,3200]{2,0,1:T(2,128)S(1)}, f32[2,10,3200]{2,0,1:T(2,128)}, u32[]{:S(2)}) copy-start(f32[2,10,3200]{2,0,1:T(2,128)} %param.21) | copy-start | bytes 768004
  90.9 455.1 %copy-start.4 = (f32[2,10,3200]{2,0,1:T(2,128)S(1)}, f32[2,10,3200]{2,0,1:T(2,128)}, u32[]{:S(2)}) copy-start(f32[2,10,3200]{2,0,1:T(2,128)} %param.18) | copy-start | bytes 768004
  90.9 458.7 %copy-start.5 = (f32[2,50,640]{2,0,1:T(2,128)S(1)}, f32[2,50,640]{2,0,1:T(2,128)}, u32[]{:S(2)}) copy-start(f32[2,50,640]{2,0,1:T(2,128)} %param.23) | copy-start | bytes 768004
  90.9 458.7 %copy-start.6 = (f32[2,50,640]{2,0,1:T(2,128)S(1)}, f32[2,50,640]{2,0,1:T(2,128)}, u32[]{:S(2)}) copy-start(f32[2,50,640]{2,0,1:T(2,128)} %param.20) | copy-start | bytes 768004
  90.9 525.9 %all-gather.6.cloned.1.call-start = ((), (), s32[]{:S(2)}) async-start(), calls=%async_computation.1 | async-start | bytes 8320000 | tf_op jit(solution)/shard_map/all_gather | solution.py:28
  546.0 151.4 %all-gather.4.cloned.1.call-start = ((), (), s32[]{:S(2)}) async-start(), calls=%async_computation | async-start | bytes 8320000 | tf_op jit(solution)/shard_map/all_gather | solution.py:28
  548.4 228.7 %all-gather.8.cloned.1.call-start = ((), (), s32[]{:S(2)}) async-start(), calls=%async_computation.2 | async-start | bytes 8320000 | tf_op jit(solution)/shard_map/all_gather | solution.py:28
Sparse Core Ops, SparseCore 0:
  91.1 268.2 all-reduce.5
  546.1 70.7 all-gather.5
  620.3 76.9 all-gather.3
  700.1 76.9 all-gather.7
where the time goes:
time: 792 us; the launch traced here: 791 us
  waiting for transfers between devices  476 us (60%)
  blocking collectives  177 us (22%)
  local copies, waits for them, and re-layouts  110 us (14%)
  between operations  17.9 us (2%)
  other arithmetic  10.8 us (1%)
    unnamed x5, waiting for transfers between devices  266 us
    all_gather x3, waiting for transfers between devices, step(): whole = [lax.all_gather(one[0], 'dp', axis=1, tiled=True) for one in new]  210 us
    psum x1, blocking collectives, step(): squares = lax.psum(sum((jnp.sum(g * g) for g in gradients)), 'dp')  177 us
    unnamed x27, local copies, waits for them, and re-layouts  108 us
  transfers between devices with their start and end apart: 4, of which 4 were waited for; matrix products, arithmetic and copies ran while one was open for 3% of the time, Pallas kernels for 0%

commit v1 on v0

v1 whole, which is shorter than its diff:
```python
import functools

import jax
import jax.numpy as jnp
import numpy as np
from jax import lax
from jax.experimental import pallas as pl
from jax.experimental.pallas import tpu as pltpu
from jax.sharding import PartitionSpec as P

MESH = pl.DeviceIdType.MESH
BF, F32 = jnp.bfloat16, jnp.float32
ANY = pl.BlockSpec(memory_space=pl.ANY)
VM = pl.BlockSpec(memory_space=pltpu.VMEM)

CT, CD = 25, 5
GU, DN = 40, 104
ROWS = CT * GU + CD * DN
BASE = CT * GU
COUNT = 3 * 2 * 640 * 3200
PARTS = ((0, 512, (0, 1, 2)), (512, 496, (1, 2, 0)), (1008, 512, (2, 0, 1)))
H0 = 256
I0, I1, I2, I3, I4 = range(5)


def perm_gu():
    p = np.zeros((160, 160), np.float32)
    for z in range(4):
        for s in range(4):
            for r in range(10):
                p[z * 40 + s * 10 + r, s * 40 + z * 10 + r] = 1
    return p


def perm_dn():
    p = np.zeros((4 * DN, 400), np.float32)
    for z in range(4):
        for s in range(2):
            for r in range(50):
                p[z * DN + s * 50 + r, s * 200 + z * 50 + r] = 1
    return p


def dot(a, b):
    return jnp.dot(a, b, preferred_element_type=F32)


def pack_line(pg, pd, gate, up, down, out):
    d = jnp.concatenate([down[0].astype(F32), down[1].astype(F32)], axis=0).astype(BF)
    d = dot(pd, d)
    for c in range(0, CT, 2):
        n = min(2, CT - c) * 128
        cols = pl.ds(c * 128, n)
        x = jnp.concatenate([ref[s, :, cols].astype(F32) for ref in (gate, up) for s in range(2)], axis=0).astype(BF)
        y = dot(pg, x)
        for z in range(4):
            one = [y[z * GU : (z + 1) * GU, i : i + 128] for i in range(0, n, 128)]
            if c == CT - 1:
                one.append(d[z * DN : (z + 1) * DN, 0:128])
            one = jnp.concatenate(one, axis=0).astype(BF)
            out[z, c * GU : c * GU + one.shape[0], :] = one
    for c in (1, 3):
        for z in range(4):
            one = [d[z * DN : (z + 1) * DN, i * 128 : (i + 1) * 128] for i in (c, c + 1)]
            out[z, BASE + c * DN : BASE + (c + 2) * DN, :] = jnp.concatenate(one, axis=0).astype(BF)


def pack_kernel(pg_ref, pd_ref, gate, up, down, out):
    pack_line(pg_ref[...], pd_ref[...], gate, up, down, out.at[0])


def pack(pg, pd, gate, up, down):
    lines = gate.shape[1] // 40
    whole = lambda a: pl.BlockSpec(a.shape, lambda i: (0,) * a.ndim)
    return pl.pallas_call(
        pack_kernel,
        grid=(lines,),
        out_shape=jax.ShapeDtypeStruct((lines, 4, ROWS, 128), BF),
        in_specs=[whole(pg), whole(pd)]
        + [pl.BlockSpec((2, 40, 3200), lambda i: (0, i, 0))] * 2
        + [pl.BlockSpec((2, 200, 640), lambda i: (0, i, 0))],
        out_specs=pl.BlockSpec((1, 4, ROWS, 128), lambda i: (i, 0, 0, 0)),
        name="pack",
    )(pg, pd, gate, up, down)


def moments_in_kernel(*refs):
    for refs3, out in ((refs[:3], refs[6]), (refs[3:6], refs[7])):
        out[...] = jnp.zeros_like(out)
        for w in range(2):
            for c in range(CT):
                for s in range(2):
                    out[pl.ds(c * GU + w * 20 + s * 10, 10), :] = refs3[w][pl.ds(2 * c + s, 10, stride=2 * CT), :]
        for c in range(CD):
            for s in range(2):
                out[pl.ds(BASE + c * DN + s * 50, 50), :] = refs3[2][pl.ds(2 * c + s, 50, stride=2 * CD), :]


def moments_in(flat):
    return pl.pallas_call(
        moments_in_kernel,
        out_shape=[jax.ShapeDtypeStruct((ROWS, 128), F32)] * 2,
        in_specs=[VM] * 6,
        out_specs=[VM] * 2,
        name="moments_in",
    )(*flat)


def moments_out(m, v, outs):
    for one, refs3 in ((m, outs[:3]), (v, outs[3:])):
        for w in range(2):
            for c in range(CT):
                for s in range(2):
                    refs3[w][pl.ds(2 * c + s, 10, stride=2 * CT), :] = one[pl.ds(c * GU + w * 20 + s * 10, 10), :]
        for c in range(CD):
            for s in range(2):
                refs3[2][pl.ds(2 * c + s, 50, stride=2 * CD), :] = one[pl.ds(BASE + c * DN + s * 50, 50), :]


def unpack_kernel(pg_ref, pd_ref, packed, m, v, gate, up, down, *outs):
    @pl.when(pl.program_id(0) == 0)
    def _():
        moments_out(m, v, outs)

    pg, pd = pg_ref[...], pd_ref[...]
    ds = [[] for _ in range(CD)]
    for c in range(0, CT, 2):
        n = min(2, CT - c)
        extra = DN if n == 1 else 0
        got = [packed[0, z, c * GU : c * GU + n * GU + extra, :].astype(F32) for z in range(4)]
        x = [jnp.concatenate([one[i * GU : (i + 1) * GU] for one in got], axis=0) for i in range(n)]
        x = jnp.concatenate(x, axis=1) if n == 2 else x[0]
        y = dot(pg, x.astype(BF))
        for i, (ref, s) in enumerate(((gate, 0), (gate, 1), (up, 0), (up, 1))):
            ref[s, :, c * 128 : (c + n) * 128] = y[i * 40 : (i + 1) * 40].astype(BF)
        if extra:
            ds[0] = [one[GU:] for one in got]
    for c in (1, 3):
        got = [packed[0, z, BASE + c * DN : BASE + (c + 2) * DN, :].astype(F32) for z in range(4)]
        for i in range(2):
            ds[c + i] = [one[i * DN : (i + 1) * DN] for one in got]
    for c in range(CD):
        y = dot(pd, jnp.concatenate(ds[c], axis=0).astype(BF))
        for s in range(2):
            down[s, :, c * 128 : (c + 1) * 128] = y[s * 200 : (s + 1) * 200].astype(BF)


def unpack(pg, pd, packed, m, v):
    whole = lambda a: pl.BlockSpec(a.shape, lambda i: (0,) * a.ndim)
    flat = pl.BlockSpec((500, 128), lambda i: (0, 0))
    return pl.pallas_call(
        unpack_kernel,
        grid=(16,),
        out_shape=[jax.ShapeDtypeStruct((2, 640, 3200), BF)] * 2
        + [jax.ShapeDtypeStruct((2, 3200, 640), BF)]
        + [jax.ShapeDtypeStruct((500, 128), F32)] * 6,
        in_specs=[whole(pg), whole(pd), pl.BlockSpec((1, 4, ROWS, 128), lambda i: (i, 0, 0, 0)), whole(m), whole(v)],
        out_specs=[pl.BlockSpec((2, 40, 3200), lambda i: (0, i, 0))] * 2
        + [pl.BlockSpec((2, 200, 640), lambda i: (0, i, 0))]
        + [flat] * 6,
        name="unpack",
    )(pg, pd, packed, m, v)


class Part:
    pass


def step_kernel(pk, wo, m, v, wg, mo, vo, wn, gs, sq, sqr, *rest):
    bufs, sems = rest[: 3 * PART_BUFS], rest[3 * PART_BUFS :]
    recv, send, local, one_sem = sems
    rep, dp = lax.axis_index("rep"), lax.axis_index("dp")
    here = [lax.div(dp, 16), lax.rem(lax.div(dp, 4), 4), lax.rem(dp, 4)]

    def at(axis, by):
        return lax.rem(here[axis] + by + 4, 4)

    def device(axis, by):
        c = list(here)
        c[axis] = at(axis, by)
        return (rep, c[I0] * 16 + c[I1] * 4 + c[I2])

    barrier = pltpu.get_barrier_semaphore()
    for axis in range(3):
        for by in (1, 2, 3):
            pl.semaphore_signal(barrier, inc=1, device_id=device(axis, by), device_id_type=MESH)
    pl.semaphore_wait(barrier, 9)

    counter = [I0]
    started = []

    def remote(src, dst, axis, by):
        i = counter[I0]
        counter[I0] += 1
        copy = pltpu.make_async_remote_copy(
            src_ref=src, dst_ref=dst, send_sem=send.at[i], recv_sem=recv.at[i], device_id=device(axis, by), device_id_type=MESH
        )
        copy.start()
        started.append(copy)
        return copy

    parts = []
    for n, (r0, rows, order) in enumerate(PARTS):
        p = Part()
        p.r0, p.rows, p.order = r0, rows, order
        p.h = (pl.ds(r0, H0), pl.ds(r0 + H0, rows - H0))
        b = bufs[n * PART_BUFS : (n + 1) * PART_BUFS]
        (p.own0, p.own1, p.ownr, p.ownl) = b[0:4]
        p.rec = (b[4:10], b[10:16], b[16:22])
        p.keep2 = b[22:26]
        p.keep3 = b[26:30]
        p.left = [at(a, -1) for a in order]
        p.right = [at(a, 1) for a in order]
        p.far = [at(a, 2) for a in order]
        p.me = [here[a] for a in order]
        p.second = 0 if order[I1] < order[I2] else 1
        parts.append(p)

    def source(p, piece, half):
        index = [slice(None)] * 3
        index[p.order[I0]] = piece
        return pk.at[(*index, p.h[half])]

    def pick(p, ref, j):
        return ref.at[j] if p.second == 0 else ref.at[:, j]

    for n, p in enumerate(parts):
        a = p.order[I0]
        far_l, far_r, dir_l, dir_r, com_l, com_r = p.rec[I0]
        p.c_far = (remote(source(p, p.far[I0], 0), far_l, a, 1), remote(source(p, p.far[I0], 1), far_r, a, -1))
    for n, p in enumerate(parts):
        a = p.order[I0]
        far_l, far_r, dir_l, dir_r, com_l, com_r = p.rec[I0]
        p.c_dir = (remote(source(p, p.right[I0], 1), dir_l, a, 1), remote(source(p, p.left[I0], 0), dir_r, a, -1))
        p.loads = [
            pltpu.make_async_copy(src, dst, local.at[4 * n + i])
            for i, (src, dst) in enumerate(
                (
                    (source(p, p.right[I0], 0), p.ownr),
                    (source(p, p.left[I0], 1), p.ownl),
                    (source(p, p.me[I0], 0), p.own0),
                    (source(p, p.me[I0], 1), p.own1),
                )
            )
        ]
        for load in p.loads:
            load.start()

    def each(count, body):
        lax.fori_loop(0, count, lambda i, _: (body(i), None)[I1], None)

    for p in parts:
        p.c_far[I0].wait_recv()
        p.c_far[I1].wait_recv()
        p.loads[I0].wait()
        p.loads[I1].wait()
    for p in parts:
        p.c_com = []
    for jj in range(4):
        for p in parts:
            j = (p.far, p.right, p.left, p.me)[jj][I1]
            pair = []
            for got, own, to, by in ((p.rec[I0][I0], p.ownr, p.rec[I0][I4], 1), (p.rec[I0][I1], p.ownl, p.rec[I0][I4 + 1], -1)):
                got, own, to = pick(p, got, j), pick(p, own, j), pick(p, to, j)

                def add(i, got=got, own=own):
                    own[i] = (own[i].astype(F32) + got[i].astype(F32)).astype(BF)

                each(4, add)
                pair.append(remote(own, to, p.order[I0], by))
            p.c_com.append(pair)
    for p in parts:
        p.c_dir[I0].wait_recv()
        p.c_dir[I1].wait_recv()
        p.loads[I2].wait()
        p.loads[I3].wait()

    for jj in range(4):
        for p in parts:
            a = p.order[I1]
            j = (p.far, p.right, p.left, p.me)[jj][I1]
            p.c_com[jj][I0].wait_recv()
            p.c_com[jj][I1].wait_recv()
            _, _, dir_l, dir_r, com_l, com_r = p.rec[I0]
            far2_l, far2_r, dir2_l, dir2_r, _, _ = p.rec[I1]
            keep0 = {1: p.keep2[I0], 3: p.keep2[I2]}.get(jj)
            keep1 = {2: p.keep2[I1], 3: p.keep2[I3]}.get(jj)
            for own, d, c, keep in ((p.own0, dir_r, com_l, keep0), (p.own1, dir_l, com_r, keep1)):
                own, d, c = pick(p, own, j), pick(p, d, j), pick(p, c, j)

                def add(i, own=own, d=d, c=c, keep=keep):
                    total = own[i].astype(F32) + d[i].astype(F32) + c[i].astype(F32)
                    if keep is None:
                        own[i] = total.astype(BF)
                    else:
                        keep[i] = total

                each(4, add)
            if jj == 0:
                p.c_far = (remote(pick(p, p.own0, j), far2_l, a, 1), remote(pick(p, p.own1, j), far2_r, a, -1))
            elif jj == 1:
                p.c_dir = [remote(pick(p, p.own1, j), dir2_l, a, 1)]
            elif jj == 2:
                p.c_dir.append(remote(pick(p, p.own0, j), dir2_r, a, -1))

    for p in parts:
        p.c_far[I0].wait_recv()
        p.c_far[I1].wait_recv()
        p.c_com = []
    for kk in range(4):
        for p in parts:
            k = (p.far, p.right, p.left, p.me)[kk][I2]
            pair = []
            for got, keep, to, by in ((p.rec[I1][I0], p.keep2[I0], p.rec[I1][I4], 1), (p.rec[I1][I1], p.keep2[I1], p.rec[I1][5], -1)):
                got[k] = (keep[k] + got[k].astype(F32)).astype(BF)
                pair.append(remote(got.at[k], to.at[k], p.order[I1], by))
            p.c_com.append(pair)
    for p in parts:
        p.c_dir[I0].wait_recv()
        p.c_dir[I1].wait_recv()

    for kk in range(4):
        for p in parts:
            a = p.order[I2]
            k = (p.far, p.right, p.left, p.me)[kk][I2]
            p.c_com[kk][I0].wait_recv()
            p.c_com[kk][I1].wait_recv()
            _, _, dir_l, dir_r, com_l, com_r = p.rec[I1]
            far3_l, far3_r, dir3_l, dir3_r, _, _ = p.rec[I2]
            keep0 = {1: p.keep3[I0], 3: p.keep3[I2]}.get(kk)
            keep1 = {2: p.keep3[I1], 3: p.keep3[I3]}.get(kk)
            total0 = p.keep2[I2][k] + dir_r[k].astype(F32) + com_l[k].astype(F32)
            total1 = p.keep2[I3][k] + dir_l[k].astype(F32) + com_r[k].astype(F32)
            if keep0 is None:
                dir_r[k] = total0.astype(BF)
            else:
                keep0[...] = total0
            if keep1 is None:
                dir_l[k] = total1.astype(BF)
            else:
                keep1[...] = total1
            if kk == 0:
                p.c_far = (remote(dir_r.at[k], far3_l, a, 1), remote(dir_l.at[k], far3_r, a, -1))
            elif kk == 1:
                p.c_dir = [remote(dir_l.at[k], dir3_l, a, 1)]
            elif kk == 2:
                p.c_dir.append(remote(dir_r.at[k], dir3_r, a, -1))

    for p in parts:
        p.c_com = []
        for got, keep, to, by, c in (
            (p.rec[I2][I0], p.keep3[I0], p.rec[I2][I4], 1, p.c_far[I0]),
            (p.rec[I2][I1], p.keep3[I1], p.rec[I2][5], -1, p.c_far[I1]),
        ):
            c.wait_recv()
            got[...] = (keep[...] + got[...].astype(F32)).astype(BF)
            p.c_com.append(remote(got, to, p.order[I2], by))
    squares = jnp.zeros((8, 128), F32)
    for p in parts:
        for c in (*p.c_dir, *p.c_com):
            c.wait_recv()
        _, _, dir_l, dir_r, com_l, com_r = p.rec[I2]
        for keep, d, c, rows in ((p.keep3[I2], dir_r, com_l, p.h[I0]), (p.keep3[I3], dir_l, com_r, p.h[I1])):
            g = (keep[...] + d[...].astype(F32) + c[...].astype(F32)).astype(BF).astype(F32)
            gs[rows, :] = g
            squares += jnp.sum((g * g).reshape(-1, 8, 128), axis=0)

    for axis in range(3):
        sq[axis] = squares
        copies = [remote(sq.at[axis], sqr.at[axis, by - 1], axis, by) for by in (1, 2, 3)]
        for i, c in enumerate(copies):
            c.wait_recv()
            squares += sqr[axis, i]
    total = jnp.sum(squares, axis=(0, 1), keepdims=True)
    factor = jnp.minimum(1.0, 0.5 * lax.rsqrt(total / COUNT + 1e-30))

    z = here[I2]
    block = 80

    def adamw(i):
        rows = pl.ds(pl.multiple_of(i * block, block), block)
        g = gs[rows, :] * factor
        w = wo[z, rows, :].astype(F32)
        new_m = 0.9 * m[rows, :] + 0.1 * g
        new_v = 0.95 * v[rows, :] + 0.05 * g * g
        mo[rows, :] = new_m
        vo[rows, :] = new_v
        wn[rows, :] = (w - 0.02 * (new_m * lax.rsqrt(new_v + 1e-8) + 0.1 * w)).astype(BF)

    each(ROWS // block, adamw)

    keep_copy = pltpu.make_async_copy(wn, wg.at[here[I0], here[I1], here[I2]], one_sem)
    keep_copy.start()

    def place(p, i, j, k, half):
        index = [None] * 3
        for a, value in zip(p.order, (i, j, k)):
            index[a] = slice(None) if value is None else value
        return wg.at[(*index, p.h[half])]

    def spread(p, axis, i, j, k, src=None):
        ref = [src[h] if src else place(p, i, j, k, h) for h in range(2)]
        to = [place(p, i, j, k, h) for h in range(2)]
        a = remote(ref[I0], to[I0], axis, 1)
        b = remote(ref[I1], to[I1], axis, -1)
        c = remote(ref[I1], to[I1], axis, 1)
        d = remote(ref[I0], to[I0], axis, -1)
        return a, b, c, d

    def forward(p, axis, copies, where_left, where_right):
        copies[I0].wait_recv()
        a = remote(place(p, *where_left, 0), place(p, *where_left, 0), axis, 1)
        copies[I1].wait_recv()
        b = remote(place(p, *where_right, 1), place(p, *where_right, 1), axis, -1)
        return a, b

    for p in parts:
        src = (wn.at[p.h[I0]], wn.at[p.h[I1]])
        i, j, k = p.me
        p.s3 = spread(p, p.order[I2], i, j, k, src)
        p.s2 = {}
    for p in parts:
        i, j, k = p.me
        p.s2[I0] = spread(p, p.order[I1], i, j, k, (wn.at[p.h[I0]], wn.at[p.h[I1]]))
    for p in parts:
        i, j, k = p.me
        p.f3 = forward(p, p.order[I2], p.s3, (i, j, p.left[I2]), (i, j, p.right[I2]))
    for p in parts:
        i, j, k = p.me
        p.s3[I2].wait_recv()
        p.s3[I3].wait_recv()
        p.s2[I1] = spread(p, p.order[I1], i, j, p.left[I2])
        p.s2[I2] = spread(p, p.order[I1], i, j, p.right[I2])
    keep_copy.wait()
    for p in parts:
        i, j, k = p.me
        p.f3[I0].wait_recv()
        p.f3[I1].wait_recv()
        p.s2[I3] = spread(p, p.order[I1], i, j, p.far[I2])
        p.f2 = {}
        p.s1, p.f1 = {}, {}
    for p in parts:
        i, j, k = p.me
        p.s1[I0] = spread(p, p.order[I0], i, j, None)
    for kk in range(4):
        for p in parts:
            i, j, _ = p.me
            k = (p.me, p.left, p.right, p.far)[kk][I2]
            p.f2[kk] = forward(p, p.order[I1], p.s2[kk], (i, p.left[I1], k), (i, p.right[I1], k))
    for p in parts:
        for kk in range(4):
            p.s2[kk][I2].wait_recv()
            p.s2[kk][I3].wait_recv()
        i, j, _ = p.me
        p.s1[I1] = spread(p, p.order[I0], i, p.left[I1], None)
        p.s1[I2] = spread(p, p.order[I0], i, p.right[I1], None)
    for p in parts:
        for kk in range(4):
            p.f2[kk][I0].wait_recv()
            p.f2[kk][I1].wait_recv()
        i, j, _ = p.me
        p.s1[I3] = spread(p, p.order[I0], i, p.far[I1], None)
    for jj in range(4):
        for p in parts:
            j = (p.me, p.left, p.right, p.far)[jj][I1]
            p.f1[jj] = forward(p, p.order[I0], p.s1[jj], (p.left[I0], j, None), (p.right[I0], j, None))
    for p in parts:
        for jj in range(4):
            for c in (*p.s1[jj][2:], *p.f1[jj]):
                c.wait_recv()
    for c in started:
        c.wait_send()


PART_BUFS = 30
COPIES = 3 * 30 + 9 + 3 * (6 + 24 + 24)


def step(pk, wo, m, v):
    bufs = []
    for r0, rows, order in PARTS:
        h = (H0, rows - H0)
        big = lambda half, t=BF: pltpu.VMEM((4, 4, h[half], 128), t)
        mid = lambda half, t=BF: pltpu.VMEM((4, h[half], 128), t)
        low = lambda half, t=BF: pltpu.VMEM((h[half], 128), t)
        bufs += [big(0), big(1), big(0), big(1)]
        for kind in (big, mid, low):
            bufs += [kind(0), kind(1), kind(1), kind(0), kind(0), kind(1)]
        for kind in (mid, low):
            bufs += [kind(0, F32), kind(1, F32), kind(0, F32), kind(1, F32)]
    return pl.pallas_call(
        step_kernel,
        out_shape=[
            jax.ShapeDtypeStruct((4, 4, 4, ROWS, 128), BF),
            jax.ShapeDtypeStruct((ROWS, 128), F32),
            jax.ShapeDtypeStruct((ROWS, 128), F32),
        ],
        in_specs=[ANY, VM, VM, VM],
        out_specs=[ANY, VM, VM],
        scratch_shapes=[
            pltpu.VMEM((ROWS, 128), BF),
            pltpu.VMEM((ROWS, 128), F32),
            pltpu.VMEM((3, 8, 128), F32),
            pltpu.VMEM((3, 3, 8, 128), F32),
            *bufs,
            pltpu.SemaphoreType.DMA((COPIES,)),
            pltpu.SemaphoreType.DMA((COPIES,)),
            pltpu.SemaphoreType.DMA((12,)),
            pltpu.SemaphoreType.DMA,
        ],
        compiler_params=pltpu.CompilerParams(collective_id=0, has_side_effects=True, vmem_limit_bytes=60 * 1024 * 1024),
        name="step",
    )(pk, wo, m, v)


def flat_of(x):
    layers, rows, columns = x.shape
    x = x.transpose(1, 0, 2).reshape(rows, layers, columns // 128, 128).transpose(0, 2, 1, 3)
    return x.reshape(500, 128)


def flat_to(x, shape):
    layers, rows, columns = shape
    x = x.reshape(rows, columns // 128, layers, 128).transpose(0, 2, 1, 3).reshape(rows, layers, columns)
    return x.transpose(1, 0, 2)


def solution(mesh):
    def run(*arrays):
        terms, weights, m, v = (arrays[i : i + 3] for i in (0, 3, 6, 9))
        pg, pd = perm_gu(), perm_dn()
        c = lambda a: jnp.asarray(a, BF)
        packed = pack(c(pg), c(pd), *[t[0] for t in terms])
        line = lax.div(lax.axis_index("dp"), 4)
        lines = [lax.dynamic_slice_in_dim(w, line * n, n, 1) for w, n in zip(weights, (40, 40, 200))]
        own = pack(c(pg), c(pd), *lines)[0]
        pm, pv = moments_in([flat_of(x) for x in (*m, *v)])
        wg, mo, vo = step(packed.reshape(4, 4, 4, ROWS, 128), own, pm, pv)
        outs = unpack(c(pg.T), c(pd.T), wg.reshape(16, 4, ROWS, 128), mo, vo)
        return (*outs[:3], *[flat_to(x, one.shape) for x, one in zip(outs[3:], (*m, *v))])

    all_of, cut = P(None, None, None), P(None, "dp", None)
    return jax.shard_map(
        run,
        mesh=mesh,
        in_specs=(P(("rep", "dp"), None, None, None),) * 3 + (all_of,) * 3 + (cut,) * 6,
        out_specs=(P("rep", None, None),) * 3 + (P("rep", "dp", None),) * 6,
        check_vma=False,
    )
```

time: 792 us -> 295 us (0.37)
  waiting for transfers between devices: 476 us -> 0 us
  Pallas kernels: 0 us -> 265 us
  blocking collectives: 177 us -> 0 us
  local copies, waits for them, and re-layouts: 110 us -> 27.2 us
  between operations: 17.9 us -> 0.75 us
  other arithmetic: 10.8 us -> 0 us
    unnamed x5 -> x0, waiting for transfers between devices: 266 us -> none
    pallas_call x0 -> x5, Pallas kernels: none -> 265 us  [the longest x1 205 us: step(): pl.pallas_call(step_kernel, out_shape=[jax.ShapeDtypeStruct((4, 4, 4, ROW...]
    all_gather x3 -> x0, waiting for transfers between devices: 210 us -> none  [step(): whole = [lax.all_gather(one[0], 'dp', axis=1, tiled=True) for one in new]]
    psum x1 -> x0, blocking collectives: 177 us -> none  [step(): squares = lax.psum(sum((jnp.sum(g * g) for g in gradients)), 'dp')]
    unnamed x27 -> x2, local copies, waits for them, and re-layouts: 108 us -> 0.01 us
    reshape x0 -> x18, local copies, waits for them, and re-layouts: none -> 22 us  [the longest x6 10.7 us: flat_to(): x.reshape(rows, columns // 128, layers, 128).transpose(0, 2, 1, 3)]
  transfers between devices with their start and end apart: 4 -> 0, of which waited for: 4 -> 0; matrix products, arithmetic and copies ran while one was open for 3% -> 0% of each run, Pallas kernels for 0% -> 0%
where the time goes in v1:
time: 295 us; the launch traced here: 293 us
  Pallas kernels  265 us (90%)
  local copies, waits for them, and re-layouts  27.2 us (9%)
    pallas_call x1, Pallas kernels, step(): pl.pallas_call(step_kernel, out_shape=[jax.ShapeDtypeStruct((4, 4, 4, ROW...  205 us
    pallas_call x2, Pallas kernels, pack(): pl.pallas_call(pack_kernel, grid=(lines,), out_shape=jax.ShapeDtypeStruct...  30.2 us
    pallas_call x1, Pallas kernels, unpack(): pl.pallas_call(unpack_kernel, grid=(16,), out_shape=[jax.ShapeDtypeStruct...  27.1 us
    reshape x6, local copies, waits for them, and re-layouts, flat_to(): x.reshape(rows, columns // 128, layers, 128).transpose(0, 2, 1, 3)  10.7 us
    reshape x6, local copies, waits for them, and re-layouts, flat_of(): x.transpose(1, 0, 2).reshape(rows, layers, columns // 128, 128)  6.07 us

profile of v1, /device:TPU:0, one launch (start us, length us, event | category | flops | bytes accessed | tf_op | source)
XLA Modules:
  0.0 293.2 jit_solution(2972286101020667408)
XLA Ops:
  0.7 1.2 reshape.97
  2.1 0.9 reshape.98.refs_0_
  3.0 1.2 reshape.99
  4.3 0.9 reshape.100.refs_1_
  5.2 1.2 reshape.103
  6.6 0.9 reshape.104.refs_3_
  7.5 1.2 reshape.105
  8.8 0.9 reshape.106.refs_4_
  9.7 1.2 reshape.101
  11.0 0.9 reshape.102.refs_2_
  12.2 0.9 reshape.108.refs_5_
  13.1 2.9 moments_in.1
  16.0 1.9 constant_dynamic-slice_fusion.down
  17.9 2.2 constant_dynamic-slice_fusion.1
  20.1 3.4 %pack.3 = bf16[1,4,1520,128]{3,2,1,0:T(8,128)(2,1)} custom-call(bf16[160,160]{1,0:T(8,128)(2,1)} %constant.24.clone.pg_ref, bf16[416,400]{1,0:T(8,128)(2,1)} %constant.25.clone.pd_ref, bf16[2,40,3200]{2,1,0:T(8,128)(2,1)} %get-tuple-element.38.gate, bf16[2,40,3200]{2,1,0:T(8,128)(2,1)} %get-tuple-element.37.up, ...), custom_call_target="tpu_custom_call" | custom-call | tf_op jit(solution)/shard_map/pack/pallas_call | solution.py:75
  23.5 26.8 %pack.2 = bf16[16,4,1520,128]{3,2,1,0:T(8,128)(2,1)} custom-call(bf16[160,160]{1,0:T(8,128)(2,1)} %constant.24.clone.pg_ref, bf16[416,400]{1,0:T(8,128)(2,1)} %constant.25.clone.pd_ref, bf16[2,640,3200]{2,1,0:T(8,128)(2,1)} %bitcast.50, bf16[2,640,3200]{2,1,0:T(8,128)(2,1)} %bitcast.51, bf16[2,3200,640]{2,1,0:T(8,128)(2,1)} %bitcast.52), custom_call_target="tpu_custom_call" | custom-call | tf_op jit(solution)/shard_map/pack/pallas_call | solution.py:75
  50.3 205.0 %step.1 = (bf16[4,4,4,1520,128]{4,3,2,1,0:T(8,128)(2,1)}, f32[1520,128]{1,0:T(8,128)}, f32[1520,128]{1,0:T(8,128)}) custom-call(bf16[4,4,4,1520,128]{4,3,2,1,0:T(8,128)(2,1)} %bitcast.48, bf16[4,1520,128]{2,1,0:T(8,128)(2,1)} %bitcast.53, f32[1520,128]{1,0:T(8,128)} %get-tuple-element.23.m, f32[1520,128]{1,0:T(8,128)} %get-tuple-element.24.v), custom_call_target="tpu_custom_call" | custom-call | tf_op jit(solution)/shard_map/step/pallas_call | solution.py:491
  255.4 27.1 %unpack.1 = (bf16[2,640,3200]{2,1,0:T(8,128)(2,1)}, bf16[2,640,3200]{2,1,0:T(8,128)(2,1)}, bf16[2,3200,640]{2,1,0:T(8,128)(2,1)}, f32[500,128]{1,0:T(8,128)}, f3...) custom-call(bf16[160,160]{1,0:T(8,128)(2,1)} %constant.24.clone.pg_r, ...), custom_call_target="tpu_custom_call" | custom-call | tf_op jit(solution)/shard_map/unpack/pallas_call | solution.py:151
  282.5 1.8 reshape.110
  284.3 1.8 reshape.112
  286.1 1.8 reshape.114
  287.9 1.8 reshape.116
  289.7 1.8 reshape.118
  291.4 1.8 reshape.120
  (9 shorter events, 1.3 us)
Async XLA Ops:
  0.6 11.3 %copy-start = (f32[2,50,640]{2,0,1:T(2,128)S(1)}, f32[2,50,640]{2,0,1:T(2,128)}, u32[]{:S(2)}) copy-start(f32[2,50,640]{2,0,1:T(2,128)} %param.29) | copy-start | bytes 768004

commit v2 on v0

v2 whole, which is shorter than its diff:
```python
import jax
import jax.numpy as jnp
import numpy as np
from jax import lax
from jax.experimental import pallas as pl
from jax.experimental.pallas import tpu as pltpu
from jax.sharding import PartitionSpec as P

MESH = pl.DeviceIdType.MESH
BF, F32 = jnp.bfloat16, jnp.float32
ANY = pl.BlockSpec(memory_space=pl.ANY)
VM = pl.BlockSpec(memory_space=pltpu.VMEM)
LANES = 128
X, Y, Z = range(3)
FIRST, SECOND, THIRD = range(3)
LEFT, RIGHT, FAR, ME = -1, 1, 2, 0
LAYERS = (0, 1)
COUNT = 3 * 2 * 640 * 3200

ROWS = 504
HALF = (256, 248)
SPAN = (pl.ds(0, 256), pl.ds(256, 248))
QUAD, PAIR, TAIL = 80, 40, 24
TALL = 104
ORDERS = ((X, Y, Z), (Y, Z, X), (Z, X, Y))
PARTS = range(3)
MANY = 9
SIDE, RING, GRID = 4, range(4), (4, 4, 4)


def perms():
    wide, last = np.zeros((160, 160), np.float32), np.zeros((96, 80), np.float32)
    even, odd = np.zeros((416, 400), np.float32), np.zeros((416, 400), np.float32)
    for z in RING:
        for r in range(10):
            for s in RING:
                wide[z * PAIR + s * 10 + r, s * 40 + z * 10 + r] = 1
            for s in LAYERS:
                last[z * TAIL + s * 10 + r, s * 40 + z * 10 + r] = 1
        for r in range(50):
            for s in LAYERS:
                even[z * TALL + s * 50 + r, s * 200 + z * 50 + r] = 1
                odd[z * TALL + 4 + s * 50 + r, s * 200 + z * 50 + r] = 1
    return wide, last, even, odd


def wide_rows(tile, layer):
    group, within = divmod(tile, 4)
    return group * QUAD + within % 2 * PAIR + within // 2 * 20 + layer * 10


def tall_rows(tile, layer):
    return tile % 3 * 200 + tile // 3 * 100 + layer * 50


def dot(a, b):
    return jnp.dot(a, b.astype(BF), preferred_element_type=F32)


def stack(values, axis=0):
    return jnp.concatenate(values, axis=axis)


def put(out, z, first, value):
    cut = HALF[0]
    end = first + value.shape[0]
    value = value.astype(BF) if first >= cut or end <= cut else value
    if first >= cut:
        out[1][z, first - cut : end - cut, :] = value
    elif end <= cut:
        out[0][z, first:end, :] = value
    else:
        out[0][z, first:cut, :] = value[: cut - first].astype(BF)
        out[1][z, : end - cut, :] = value[cut - first :].astype(BF)


def get(ref, z, first, end):
    cut = HALF[0]
    low, high = first // 16 * 16, -(-end // 16) * 16
    if low >= cut:
        value = ref[1][z, low - cut : min(high, ROWS) - cut, :].astype(F32)
    elif high <= cut:
        value = ref[0][z, low:high, :].astype(F32)
    else:
        value = stack([ref[0][z, low:cut, :].astype(F32), ref[1][z, : min(high, ROWS) - cut, :].astype(F32)])
    return value[first - low : end - low]


def pack_wide(wide, last, src, out):
    for first in range(0, 3072, 4 * LANES):
        x = [src[s, :, pl.ds(first + two * 2 * LANES, 2 * LANES)].astype(F32) for two in LAYERS for s in LAYERS]
        y = dot(wide, stack(x))
        for z in RING:
            one = y[z * PAIR : (z + 1) * PAIR]
            put(out, z, first // (4 * LANES) * QUAD, stack([one[:, :LANES], one[:, LANES:]]))
    y = dot(last, stack([src[s, :, pl.ds(3072, LANES)].astype(F32) for s in LAYERS]))
    for z in RING:
        put(out, z, ROWS - TAIL, y[z * TAIL : (z + 1) * TAIL])


def unpack_wide(wide, last, block, write):
    for first in range(0, 3072, 4 * LANES):
        row = first // (4 * LANES) * QUAD
        got = [get(block, z, row, row + QUAD) for z in RING]
        x = stack([stack([one[:PAIR] for one in got]), stack([one[PAIR:] for one in got])], 1)
        y = dot(wide, x)
        for two in LAYERS:
            for s in LAYERS:
                at = (two * 2 + s) * 40
                write(s, pl.ds(first + two * 2 * LANES, 2 * LANES), y[at : at + 40])
    y = dot(last, stack([get(block, z, ROWS - TAIL, ROWS) for z in RING]))
    for s in LAYERS:
        write(s, pl.ds(3072, LANES), y[s * 40 : (s + 1) * 40])


def pack_tall(even, odd, src, out):
    def columns(a, b):
        return stack([src[s, :, a * LANES : b * LANES].astype(F32) for s in LAYERS])

    a, b = dot(even, columns(0, 3)), dot(odd, columns(3, 5))
    for z in RING:
        one, rows = [], slice(z * TALL, (z + 1) * TALL)
        for pair in range(3):
            u = a[rows, pair * LANES : (pair + 1) * LANES]
            if pair == 2:
                one.append(u)
            else:
                v = b[rows, pair * LANES : (pair + 1) * LANES]
                one += [u[:96], u[96:] + v[:8], v[8:]]
        put(out, z, 0, stack(one))


def unpack_tall(even, odd, block, write):
    for tile in range(5):
        first = tall_rows(tile, 0) - tile // 3 * 4
        x = stack([get(block, z, first, first + TALL) for z in RING])
        y = dot((even, odd)[tile // 3], x)
        for s in LAYERS:
            write(s, pl.ds(tile * LANES, LANES), y[s * 200 : (s + 1) * 200])


def each(count, body, start=0):
    lax.fori_loop(start, count, lambda i, _: (body(i), None)[1], None)


class Part:
    pass


class Place:
    def __init__(self, partners):
        self.rep, dp = lax.axis_index("rep"), lax.axis_index("dp")
        self.here = (lax.div(dp, 16), lax.rem(lax.div(dp, 4), 4), lax.rem(dp, 4))
        barrier = pltpu.get_barrier_semaphore()
        for axis in (X, Y, Z):
            for by in partners:
                pl.semaphore_signal(barrier, inc=1, device_id=self.device(axis, by), device_id_type=MESH)
        pl.semaphore_wait(barrier, 3 * len(partners))
        self.count = 0
        self.started = []

    def at(self, axis, by):
        return lax.rem(self.here[axis] + (by + 4), 4)

    def device(self, axis, by):
        c = [self.at(a, by if a == axis else ME) for a in (X, Y, Z)]
        return (self.rep, c[X] * 16 + c[Y] * 4 + c[Z])

    def copy(self, src, dst, axis, by, send, recv):
        return pltpu.make_async_remote_copy(
            src_ref=src, dst_ref=dst, send_sem=send, recv_sem=recv, device_id=self.device(axis, by), device_id_type=MESH
        )

    def send(self, src, dst, axis, by, sems):
        copy = self.copy(src, dst, axis, by, sems[0].at[self.count], sems[1].at[self.count])
        self.count += 1
        copy.start()
        self.started.append(copy)
        return copy

    def parts(self):
        made = []
        for n in PARTS:
            p = Part()
            p.n, p.order = n, ORDERS[n]
            p.second = ORDERS[n][SECOND] < ORDERS[n][THIRD]
            made.append(p)
        return made

    def index(self, p, i, j, k):
        index = [None] * 3
        for a, value in zip(p.order, (i, j, k)):
            index[a] = slice(None) if value is None else value
        return tuple(index)


def step_kernel(*refs):
    grads, weights, m_in, v_in, mats = (refs[i:j] for i, j in ((0, 3), (3, 6), (6, 9), (9, 12), (12, 16)))
    new0, new1, mo, vo = refs[16:20]
    scratch = refs[20:]
    lines, scratch = scratch[:3], scratch[3:]
    own, scratch = [scratch[2 * n : 2 * n + 2] for n in PARTS], scratch[6:]
    packed, scratch = [scratch[2 * n : 2 * n + 2] for n in PARTS], scratch[6:]
    rec, scratch = [[scratch[18 * n + 6 * f : 18 * n + 6 * f + 6] for f in PARTS] for n in PARTS], scratch[54:]
    gs, sq, sqr, send, recv, early_send, early_recv, load_sem = scratch
    sems = (send, recv)

    place = Place((RIGHT, FAR, LEFT))
    at = place.at
    parts = place.parts()
    mats = [one[...] for one in mats]

    def line_copies(srcs, line, slot):
        for n, (src, height) in enumerate(zip(srcs, (40, 40, 200))):
            rows = pl.ds(pl.multiple_of(line * height, 8), height)
            yield pltpu.make_async_copy(src.at[:, rows, :], lines[n].at[slot], load_sem.at[slot, n])

    def pack(slot, outs):
        for n in PARTS:
            src = lines[n].at[slot]
            if n < 2:
                pack_wide(*mats[:2], src, outs[n])
            else:
                pack_tall(*mats[2:], src, outs[n])

    def distance(u):
        return lax.rem(6 - u + 3 * lax.div(u, 2) - 2 * lax.div(u, 3), 4)

    def where(t):
        u, w = lax.div(t, 4), lax.rem(t, 4)
        return w, lax.rem(u + w, 4)

    def line_of(t):
        a, b = where(t)
        return at(X, distance(a)), at(Y, distance(b))

    def start_line(t):
        x, y = line_of(t)
        for c in line_copies(grads, x * 4 + y, lax.rem(t, 2)):
            c.start()

    start_line(0)
    start_line(1)

    def first_copies(p, got, kind, piece, block):
        far_l, far_r, dir_l, dir_r = rec[p.n][FIRST][:4]
        axis = p.order[FIRST]
        todo = (
            ((0, far_l, RIGHT, 0), (1, far_r, LEFT, 1)),
            ((1, dir_l, RIGHT, 2),),
            ((0, dir_r, LEFT, 3),),
        )[kind]
        for half, to, by, s in todo:
            place.copy(got[half].at[piece], to.at[block], axis, by, early_send.at[p.n, s], early_recv.at[p.n, s]).start()

    def one_line(t):
        slot = lax.rem(t, 2)
        a, b = where(t)
        x, y = line_of(t)
        for c in line_copies(grads, x * 4 + y, slot):
            c.wait()
        pack(slot, [[half.at[x, y] for half in packed[n]] for n in PARTS])

        @pl.when(t < 14)
        def _():
            start_line(t + 2)

        for kind in range(3):

            @pl.when(a == kind)
            def _():
                first_copies(parts[0], packed[0], kind, (x, y), y)

            @pl.when(b == kind)
            def _():
                first_copies(parts[1], packed[1], kind, (x, y), x)

            first_copies(parts[2], packed[2], kind, (x, y, at(Z, (FAR, RIGHT, LEFT)[kind])), (x, y))

    each(16, one_line)

    for c in line_copies(weights, at(X, ME) * 4 + at(Y, ME), 0):
        c.start()
    for new, old in ((mo, m_in), (vo, v_in)):
        new[:, 480:ROWS, :] = jnp.zeros((3, TAIL, LANES), F32)
        for n in PARTS:
            rows, height, tiles = (tall_rows, 50, 5) if n == 2 else (wide_rows, 10, 25)
            for tile in range(tiles):
                for s in LAYERS:
                    new[n, pl.ds(rows(tile, s), height), :] = old[n][:, s, tile * LANES : (tile + 1) * LANES]
    for c in line_copies(weights, at(X, ME) * 4 + at(Y, ME), 0):
        c.wait()
    pack(0, own)

    def early_wait(p, s):
        ref = rec[p.n][FIRST][s]
        place.copy(ref, ref, p.order[FIRST], LEFT, early_send.at[p.n, s], early_recv.at[p.n, s]).wait_recv()

    def block(p, ref, j, k):
        return ref.at[(j, k) if p.second else (k, j)]

    def whole(p, ref, j):
        return ref.at[j] if p.second else ref.at[:, j]

    def total(refs):
        value = refs[0][...].astype(F32)
        for ref in refs[1:]:
            value = value + ref[...].astype(F32)
        return value

    def terms1(p, half, piece, j, k):
        return [packed[p.n][half].at[place.index(p, piece, j, k)]]

    def terms2(p, half, j, k):
        _, _, dir_l, dir_r, com_l, com_r = rec[p.n][FIRST]
        more = ((dir_r, com_l), (dir_l, com_r))[half]
        return terms1(p, half, p.me[FIRST], j, k) + [block(p, ref, j, k) for ref in more]

    def terms3(p, half, k):
        _, _, dir_l, dir_r, com_l, com_r = rec[p.n][SECOND]
        more = ((dir_r, com_l), (dir_l, com_r))[half]
        return terms2(p, half, p.me[SECOND], k) + [ref.at[k] for ref in more]

    STEPS = (FAR, RIGHT, LEFT, ME)
    LEAVES = {
        FAR: ((0, 3, 0, RIGHT), (1, 2, 1, LEFT)),
        RIGHT: ((1, 2, 2, RIGHT),),
        LEFT: ((0, 3, 3, LEFT),),
        ME: (),
    }
    COMBINE = ((0, 0, 4, RIGHT), (1, 1, 5, LEFT))

    for p in parts:
        p.me = [at(a, ME) for a in p.order]
        p.to = {by: [at(a, by) for a in p.order] for by in STEPS}
        early_wait(p, 0)
        early_wait(p, 1)
        p.com = {}
    for by in STEPS:
        for p in parts:
            j = p.to[by][SECOND]
            p.com[by] = []
            for half, got, to, way in COMBINE:
                got, to = (rec[p.n][FIRST][i] for i in (got, to))

                def add(k):
                    ref = block(p, got, j, k)
                    ref[...] = total(terms1(p, half, p.to[way][FIRST], j, k) + [ref]).astype(BF)

                each(SIDE, add)
                p.com[by].append(place.send(whole(p, got, j), whole(p, to, j), p.order[FIRST], way, sems))
    for p in parts:
        early_wait(p, 2)
        early_wait(p, 3)
        p.next = {}

    for by in STEPS:
        for p in parts:
            j = p.to[by][SECOND]
            for c in p.com[by]:
                c.wait_recv()
            for half, slot, target, way in LEAVES[by]:
                ref = rec[p.n][FIRST][slot]

                def add(k):
                    block(p, ref, j, k)[...] = total(terms2(p, half, j, k)).astype(BF)

                each(SIDE, add)
                p.next[target] = place.send(whole(p, ref, j), rec[p.n][SECOND][target], p.order[SECOND], way, sems)

    for p in parts:
        p.next[0].wait_recv()
        p.next[1].wait_recv()
    for by in STEPS:
        for p in parts:
            k = p.to[by][THIRD]
            p.com[by] = []
            for half, got, to, way in COMBINE:
                got, to = (rec[p.n][SECOND][i].at[k] for i in (got, to))
                got[...] = total(terms2(p, half, p.to[way][SECOND], k) + [got]).astype(BF)
                p.com[by].append(place.send(got, to, p.order[SECOND], way, sems))
    for p in parts:
        p.next[2].wait_recv()
        p.next[3].wait_recv()
        p.next = {}

    for by in STEPS:
        for p in parts:
            k = p.to[by][THIRD]
            for c in p.com[by]:
                c.wait_recv()
            for half, slot, target, way in LEAVES[by]:
                ref = rec[p.n][SECOND][slot].at[k]
                ref[...] = total(terms3(p, half, k)).astype(BF)
                p.next[target] = place.send(ref, rec[p.n][THIRD][target], p.order[THIRD], way, sems)

    for p in parts:
        p.com = []
        for half, got, to, way in COMBINE:
            p.next[got].wait_recv()
            got, to = (rec[p.n][THIRD][i] for i in (got, to))
            got[...] = total(terms3(p, half, p.to[way][THIRD]) + [got]).astype(BF)
            p.com.append(place.send(got, to, p.order[THIRD], way, sems))
    squares = jnp.zeros((8, LANES), F32)
    for p in parts:
        for c in (p.next[2], p.next[3], *p.com):
            c.wait_recv()
        _, _, dir_l, dir_r, com_l, com_r = rec[p.n][THIRD]
        for half in LAYERS:
            g = total(terms3(p, half, p.me[THIRD]) + [(dir_r, dir_l)[half], (com_l, com_r)[half]]).astype(BF).astype(F32)
            gs[p.n, SPAN[half], :] = g
            squares += jnp.sum((g * g).reshape(-1, 8, LANES), axis=0)

    for axis in (X, Y, Z):
        sq[axis] = squares
        copies = [place.send(sq.at[axis], sqr.at[axis, i], axis, by, sems) for i, by in enumerate((RIGHT, FAR, LEFT))]
        for i, c in enumerate(copies):
            c.wait_recv()
            squares += sqr[axis, i]
    squares = jnp.sum(squares, axis=(0, 1), keepdims=True)
    factor = jnp.minimum(1.0, 0.5 * lax.rsqrt(squares / COUNT + 1e-30))

    for n in PARTS:
        for half in LAYERS:
            rows = SPAN[half]
            g = gs[n, rows, :] * factor
            w = own[n][half][at(Z, ME)].astype(F32)
            m = 0.9 * mo[n, rows, :] + 0.1 * g
            v = 0.95 * vo[n, rows, :] + 0.05 * g * g
            mo[n, rows, :] = m
            vo[n, rows, :] = v
            (new0, new1)[half][n] = (w - 0.02 * (m * lax.rsqrt(v + 1e-8) + 0.1 * w)).astype(BF)

    for c in place.started:
        c.wait_send()
    for p in parts:
        for s in RING:
            ref = rec[p.n][FIRST][s]
            place.copy(ref, ref, p.order[FIRST], LEFT, early_send.at[p.n, s], early_recv.at[p.n, s]).wait_send()


def halves(*lead, dtype=BF):
    return [pltpu.VMEM((*lead, h, LANES), dtype) for h in HALF]


def shape(*dims, dtype=BF):
    return jax.ShapeDtypeStruct(dims, dtype)


def step(grads, weights, m, v, mats):
    rec = []
    for lead in ((4, 4), (4,), ()):
        a, b = halves(*lead)
        rec += [a, b, b, a, a, b]
    copies = 87
    return pl.pallas_call(
        step_kernel,
        out_shape=[shape(3, HALF[0], LANES), shape(3, HALF[1], LANES)] + [shape(3, ROWS, LANES, dtype=F32)] * 2,
        in_specs=[ANY] * 6 + [VM] * 10,
        out_specs=[VM] * 4,
        scratch_shapes=[
            pltpu.VMEM((2, 2, 40, 3200), BF),
            pltpu.VMEM((2, 2, 40, 3200), BF),
            pltpu.VMEM((2, 2, 200, 640), BF),
            *halves(4) * 3,
            *halves(*GRID) * 3,
            *rec * 3,
            pltpu.VMEM((3, ROWS, LANES), F32),
            pltpu.VMEM((3, 8, LANES), F32),
            pltpu.VMEM((3, 3, 8, LANES), F32),
            pltpu.SemaphoreType.DMA((copies,)),
            pltpu.SemaphoreType.DMA((copies,)),
            pltpu.SemaphoreType.DMA((3, 4)),
            pltpu.SemaphoreType.DMA((3, 4)),
            pltpu.SemaphoreType.DMA((2, 3)),
        ],
        compiler_params=pltpu.CompilerParams(collective_id=0, has_side_effects=True, vmem_limit_bytes=67043328),
        name="step",
    )(*grads, *weights, *m, *v, *mats)


def gather_kernel(*refs):
    new, moments, mats, outs, moved = (refs[i:j] for i, j in ((0, 2), (2, 4), (4, 8), (8, 11), (11, 17)))
    scratch = refs[17:]
    got = [scratch[2 * n : 2 * n + 2] for n in PARTS]
    send, recv, late_send, late_recv = scratch[6:]
    sems = (send, recv)

    place = Place((RIGHT, LEFT))
    at = place.at
    parts = place.parts()
    for p in parts:
        p.me, p.left, p.right, p.far = ([at(a, by) for a in p.order] for by in (ME, LEFT, RIGHT, FAR))
        p.steps = (p.me, p.left, p.right, p.far)

    def ref_of(p, half, i, j, k):
        return got[p.n][half].at[place.index(p, i, j, k)]

    def spread(p, axis, i, j, k, mine=False):
        to = [ref_of(p, h, i, j, k) for h in LAYERS]
        src = [new[h].at[p.n] for h in LAYERS] if mine else to
        return [place.send(src[h], to[h], axis, by, sems) for h, by in ((0, RIGHT), (1, LEFT), (1, RIGHT), (0, LEFT))]

    def forward(p, axis, copies, from_left, from_right):
        copies[0].wait_recv()
        left = ref_of(p, 0, *from_left)
        a = place.send(left, left, axis, RIGHT, sems)
        copies[1].wait_recv()
        right = ref_of(p, 1, *from_right)
        return a, place.send(right, right, axis, LEFT, sems)

    def arrived(*copies):
        for c in copies:
            c.wait_recv()

    def chunk(p, axis_place, step):
        i, value = axis_place, step
        return (i, None, value) if p.n == 1 else (i, value, None)

    def late(p, jj, e, half, index, way):
        ref = ref_of(p, half, *index)
        return place.copy(ref, ref, p.order[FIRST], way, late_send.at[p.n, jj, e], late_recv.at[p.n, jj, e])

    def along(p):
        return p.order[THIRD if p.n == 1 else SECOND]

    def last_spread(p, jj, by):
        index = chunk(p, p.me[FIRST], at(along(p), by))
        for e, (h, way) in enumerate(((0, RIGHT), (1, LEFT), (1, RIGHT), (0, LEFT))):
            late(p, jj, e, h, index, way).start()

    for p in parts:
        p.s3 = spread(p, p.order[THIRD], *p.me, mine=True)
    for p in parts:
        p.s2, p.f2 = [spread(p, p.order[SECOND], *p.me, mine=True)], []
    for p in parts:
        for h in LAYERS:
            ref_of(p, h, *p.me)[...] = new[h][p.n]
    for p in parts:
        i, j, k = p.me
        p.f3 = forward(p, p.order[THIRD], p.s3, (i, j, p.left[THIRD]), (i, j, p.right[THIRD]))
    for p in parts:
        arrived(*p.s3[2:])
        for k in (p.left[THIRD], p.right[THIRD]):
            p.s2.append(spread(p, p.order[SECOND], *p.me[:THIRD], k))
    for p in parts:
        arrived(*p.f3)
        p.s2.append(spread(p, p.order[SECOND], *p.me[:THIRD], p.far[THIRD]))
        if p.n != 1:
            last_spread(p, 0, ME)
    for step, by in enumerate((ME, LEFT, RIGHT, FAR)):
        for p in parts:
            i, k = p.me[FIRST], p.steps[step][THIRD]
            p.f2.append(forward(p, p.order[SECOND], p.s2[step], (i, p.left[SECOND], k), (i, p.right[SECOND], k)))
        p = parts[1]
        if step:
            arrived(*p.s2[step - 1][2:], *p.f2[step - 1])
            last_spread(p, step - 1, (ME, LEFT, RIGHT)[step - 1])
    for p in parts:
        if p.n == 1:
            arrived(*p.s2[3][2:], *p.f2[3])
            last_spread(p, 3, FAR)
        else:
            for copies in p.s2:
                arrived(*copies[2:])
            last_spread(p, 1, LEFT)
            last_spread(p, 2, RIGHT)
            for copies in p.f2:
                arrived(*copies)
            last_spread(p, 3, FAR)

    for out, one in zip((moved[:3], moved[3:]), moments):
        for n in PARTS:
            rows, height, tiles = (tall_rows, 50, 5) if n == 2 else (wide_rows, 10, 25)
            for tile in range(tiles):
                for s in LAYERS:
                    out[n][:, s, tile * LANES : (tile + 1) * LANES] = one[n, pl.ds(rows(tile, s), height), :]

    mats = [one[...] for one in mats]

    def line(p, x, y):
        block = [half.at[x, y] for half in got[p.n]]
        height = 200 if p.n == 2 else 40
        rows = pl.ds(pl.multiple_of((x * 4 + y) * height, 8), height)

        def write(layer, columns, value):
            outs[p.n][layer, rows, columns] = value.astype(BF)

        if p.n == 2:
            unpack_tall(*mats[2:], block, write)
        else:
            unpack_wide(*mats[:2], block, write)

    def distance(jj):
        return 3 * lax.rem(jj, 2) + lax.div(jj, 2) - 2 * lax.div(jj, 3)

    def last(jj):
        @pl.when(jj < 4)
        def _():
            for p in parts:
                value = at(along(p), distance(jj))
                left, right = (chunk(p, i, value) for i in (p.left[FIRST], p.right[FIRST]))
                late(p, jj, 0, 0, left, LEFT).wait_recv()
                late(p, jj, 4, 0, left, RIGHT).start()
                late(p, jj, 1, 1, right, LEFT).wait_recv()
                late(p, jj, 5, 1, right, LEFT).start()
            for p in parts:
                value = at(along(p), distance(jj))
                left, right = (chunk(p, i, value) for i in (p.left[FIRST], p.right[FIRST]))
                late(p, jj, 2, 1, left, LEFT).wait_recv()
                late(p, jj, 3, 0, right, LEFT).wait_recv()

        before = jj - 1

        @pl.when(jj > 0)
        def _():
            for p in parts:
                far = chunk(p, p.far[FIRST], at(along(p), distance(before)))
                late(p, before, 4, 0, far, LEFT).wait_recv()
                late(p, before, 5, 1, far, LEFT).wait_recv()

        def one(i):
            which = jj - lax.div(i, 3)

            @pl.when((which >= 0) & (which < 4))
            def _():
                value = distance(which)
                line(parts[0], at(X, distance(i)), at(Y, value))
                line(parts[1], at(X, value), at(Y, distance(i)))

            @pl.when(jj > 0)
            def _():
                line(parts[2], at(X, distance(before)), i)

        each(SIDE, one)

    each(5, last)

    for c in place.started:
        c.wait_send()

    def drain(jj):
        for p in parts:
            index = chunk(p, p.me[FIRST], at(along(p), distance(jj)))
            for e, h in enumerate((0, 1, 1, 0, 0, 1)):
                late(p, jj, e, h, index, LEFT).wait_send()

    each(SIDE, drain)


def gather(new, moments, mats):
    copies = 90
    wide, tall = (10, 2, 3200), (50, 2, 640)
    outs = [pltpu.VMEM((2, 640, 3200), BF)] * 2 + [pltpu.VMEM((2, 3200, 640), BF)]
    outs += [pltpu.VMEM(one, F32) for one in (wide, wide, tall)] * 2
    return pl.pallas_call(
        gather_kernel,
        out_shape=outs,
        in_specs=[VM] * 8,
        out_specs=[VM] * MANY,
        scratch_shapes=[
            *halves(*GRID) * 3,
            pltpu.SemaphoreType.DMA((copies,)),
            pltpu.SemaphoreType.DMA((copies,)),
            pltpu.SemaphoreType.DMA((3, 4, 6)),
            pltpu.SemaphoreType.DMA((3, 4, 6)),
        ],
        compiler_params=pltpu.CompilerParams(collective_id=1, has_side_effects=True, vmem_limit_bytes=30 * 2**20),
        name="gather",
    )(*new, *moments, *mats)


def finish_kernel(*refs):
    held, outs, sem = refs[:MANY], refs[MANY : 2 * MANY], refs[2 * MANY]
    copies = [pltpu.make_async_copy(a, b, sem.at[n]) for n, (a, b) in enumerate(zip(held, outs))]
    for c in copies:
        c.start()
    for c in copies:
        c.wait()


def finish(held):
    return pl.pallas_call(
        finish_kernel,
        out_shape=[shape(*one.shape, dtype=one.dtype) for one in held],
        in_specs=[VM] * MANY,
        out_specs=[ANY] * MANY,
        scratch_shapes=[pltpu.SemaphoreType.DMA((MANY,))],
        compiler_params=pltpu.CompilerParams(vmem_limit_bytes=8 * 2**20),
        name="finish",
    )(*held)


def solution(mesh):
    def run(*arrays):
        terms, weights, m, v = (arrays[i : i + 3] for i in (0, 3, 6, 9))
        swap = lambda arrays: [x.transpose(1, 0, 2) for x in arrays]
        mats = perms()
        *new, mo, vo = step([t[0] for t in terms], weights, swap(m), swap(v), [jnp.asarray(a, BF) for a in mats])
        outs = finish(gather(new, (mo, vo), [jnp.asarray(a.T, BF) for a in mats]))
        return (*outs[:3], *swap(outs[3:]))

    all_of, cut = P(None, None, None), P(None, "dp", None)
    return jax.shard_map(
        run,
        mesh=mesh,
        in_specs=(P(("rep", "dp"), None, None, None),) * 3 + (all_of,) * 3 + (cut,) * 6,
        out_specs=(P("rep", None, None),) * 3 + (P("rep", "dp", None),) * 6,
        check_vma=False,
    )
```

time: 792 us -> 240 us (0.30)
  waiting for transfers between devices: 476 us -> 0 us
  Pallas kernels: 0 us -> 238 us
  blocking collectives: 177 us -> 0 us
  local copies, waits for them, and re-layouts: 110 us -> 0 us
  between operations: 17.9 us -> 0.66 us
  other arithmetic: 10.8 us -> 0 us
    unnamed x5 -> x0, waiting for transfers between devices: 266 us -> none
    pallas_call x0 -> x3, Pallas kernels: none -> 238 us  [the longest x1 118 us: step(): pl.pallas_call(step_kernel, out_shape=[shape(3, HALF[0], LANES), shape(3,...]
    all_gather x3 -> x0, waiting for transfers between devices: 210 us -> none  [step(): whole = [lax.all_gather(one[0], 'dp', axis=1, tiled=True) for one in new]]
    psum x1 -> x0, blocking collectives: 177 us -> none  [step(): squares = lax.psum(sum((jnp.sum(g * g) for g in gradients)), 'dp')]
    unnamed x27 -> x0, local copies, waits for them, and re-layouts: 108 us -> none
  transfers between devices with their start and end apart: 4 -> 0, of which waited for: 4 -> 0; matrix products, arithmetic and copies ran while one was open for 3% -> 0% of each run, Pallas kernels for 0% -> 0%
where the time goes in v2:
time: 240 us; the launch traced here: 239 us
  Pallas kernels  238 us (99%)
    pallas_call x1, Pallas kernels, step(): pl.pallas_call(step_kernel, out_shape=[shape(3, HALF[0], LANES), shape(3,...  118 us
    pallas_call x1, Pallas kernels, gather(): pl.pallas_call(gather_kernel, out_shape=outs, in_specs=[VM] * 8, out_spec...  112 us
    pallas_call x1, Pallas kernels, finish(): pl.pallas_call(finish_kernel, out_shape=[shape(*one.shape, dtype=one.dtyp...  8.79 us

profile of v2, /device:TPU:0, one launch (start us, length us, event | category | flops | bytes accessed | tf_op | source)
XLA Modules:
  0.0 239.1 jit_solution(13455615239932799516)
XLA Ops:
  0.6 118.0 %step.1 = (bf16[3,256,128]{2,1,0:T(8,128)(2,1)}, bf16[3,248,128]{2,1,0:T(8,128)(2,1)}, f32[3,504,128]{2,1,0:T(8,128)}, f32[3,504,128]{2,1,0:T(8,128)}) custom-call(bf16[2,640,3200]{2,1,0:T(8,128)(2,1)} %bitcast.15, bf16[2,640,3200]{2,1,0:T(8,128)(2,1)} %bitcast.16, bf16[2,3200,640]{2,1,0:T(8,128)(2,1)} %bitcast.17, bf16[2,640,3200]{2,1,0:T(8,128)(2,1)} %refs_3_.1, ...), custom_call_target="tpu_custom_call" | custom-call | tf_op jit(solution)/shard_map/step/pallas_call | solution.py:456
  118.7 111.6 %gather.1 = (bf16[2,640,3200]{2,1,0:T(8,128)(2,1)S(1)}, bf16[2,640,3200]{2,1,0:T(8,128)(2,1)S(1)}, bf16[2,3200,640]{2,1,0:T(8,128)(2,1)S(1)}, f32[10,2,3200]{2,1...) custom-call(bf16[3,256,128]{2,1,0:T(8,128)(2,1)} %get-tuple-element., ...), custom_call_target="tpu_custom_call" | custom-call | tf_op jit(solution)/shard_map/gather/pallas_call | solution.py:656
  230.3 8.8 %finish.1 = (bf16[2,640,3200]{2,1,0:T(8,128)(2,1)}, bf16[2,640,3200]{2,1,0:T(8,128)(2,1)}, bf16[2,3200,640]{2,1,0:T(8,128)(2,1)}, f32[10,2,3200]{2,1,0:T(2,128)}...) custom-call(bf16[2,640,3200]{2,1,0:T(8,128)(2,1)S(1)} %get-tuple-ele, ...), custom_call_target="tpu_custom_call" | custom-call | tf_op jit(solution)/shard_map/finish/pallas_call | solution.py:683

commit v3 on v2

--- a/solution.py
+++ b/solution.py
@@ -1,6 +1,5 @@
 import jax
 import jax.numpy as jnp
-import numpy as np
 from jax import lax
 from jax.experimental import pallas as pl
 from jax.experimental.pallas import tpu as pltpu
@@ -20,41 +19,20 @@
 ROWS = 504
 HALF = (256, 248)
 SPAN = (pl.ds(0, 256), pl.ds(256, 248))
-QUAD, PAIR, TAIL = 80, 40, 24
-TALL = 104
+QUAD, TAIL = 80, 24
+GROUPS = [range(t, min(t + 4, 25)) for t in range(0, 25, 4)]
 ORDERS = ((X, Y, Z), (Y, Z, X), (Z, X, Y))
 PARTS = range(3)
 MANY = 9
 SIDE, RING, GRID = 4, range(4), (4, 4, 4)
 
 
-def perms():
-    wide, last = np.zeros((160, 160), np.float32), np.zeros((96, 80), np.float32)
-    even, odd = np.zeros((416, 400), np.float32), np.zeros((416, 400), np.float32)
-    for z in RING:
-        for r in range(10):
-            for s in RING:
-                wide[z * PAIR + s * 10 + r, s * 40 + z * 10 + r] = 1
-            for s in LAYERS:
-                last[z * TAIL + s * 10 + r, s * 40 + z * 10 + r] = 1
-        for r in range(50):
-            for s in LAYERS:
-                even[z * TALL + s * 50 + r, s * 200 + z * 50 + r] = 1
-                odd[z * TALL + 4 + s * 50 + r, s * 200 + z * 50 + r] = 1
-    return wide, last, even, odd
-
-
 def wide_rows(tile, layer):
-    group, within = divmod(tile, 4)
-    return group * QUAD + within % 2 * PAIR + within // 2 * 20 + layer * 10
+    return tile * 20 + layer * 10
 
 
 def tall_rows(tile, layer):
-    return tile % 3 * 200 + tile // 3 * 100 + layer * 50
-
-
-def dot(a, b):
-    return jnp.dot(a, b.astype(BF), preferred_element_type=F32)
+    return tile * 100 + layer * 50
 
 
 def stack(values, axis=0):
@@ -86,57 +64,40 @@
     return value[first - low : end - low]
 
 
-def pack_wide(wide, last, src, out):
-    for first in range(0, 3072, 4 * LANES):
-        x = [src[s, :, pl.ds(first + two * 2 * LANES, 2 * LANES)].astype(F32) for two in LAYERS for s in LAYERS]
-        y = dot(wide, stack(x))
+def pack_wide(src, out):
+    for group in range(7):
+        tiles = GROUPS[group]
+        x = [[src[s, :, pl.ds(t * LANES, LANES)].astype(F32) for s in LAYERS] for t in tiles]
         for z in RING:
-            one = y[z * PAIR : (z + 1) * PAIR]
-            put(out, z, first // (4 * LANES) * QUAD, stack([one[:, :LANES], one[:, LANES:]]))
-    y = dot(last, stack([src[s, :, pl.ds(3072, LANES)].astype(F32) for s in LAYERS]))
+            rows = [one[s][z * 10 : (z + 1) * 10] for one in x for s in LAYERS]
+            if len(tiles) == 1:
+                rows.append(jnp.zeros((SIDE, LANES), F32))
+            put(out, z, group * QUAD, stack(rows))
+
+
+def unpack_wide(block, write):
+    for group in range(7):
+        tiles = GROUPS[group]
+        got = [get(block, z, group * QUAD, min(ROWS, (group + 1) * QUAD)) for z in RING]
+        for n, t in enumerate(tiles):
+            for s in LAYERS:
+                row = n * 20 + s * 10
+                write(s, pl.ds(t * LANES, LANES), stack([one[row : row + 10] for one in got]))
+
+
+def pack_tall(src, out):
+    x = [[src[s, :, pl.ds(t * LANES, LANES)].astype(F32) for s in LAYERS] for t in range(5)]
     for z in RING:
-        put(out, z, ROWS - TAIL, y[z * TAIL : (z + 1) * TAIL])
-
-
-def unpack_wide(wide, last, block, write):
-    for first in range(0, 3072, 4 * LANES):
-        row = first // (4 * LANES) * QUAD
-        got = [get(block, z, row, row + QUAD) for z in RING]
-        x = stack([stack([one[:PAIR] for one in got]), stack([one[PAIR:] for one in got])], 1)
-        y = dot(wide, x)
-        for two in LAYERS:
-            for s in LAYERS:
-                at = (two * 2 + s) * 40
-                write(s, pl.ds(first + two * 2 * LANES, 2 * LANES), y[at : at + 40])
-    y = dot(last, stack([get(block, z, ROWS - TAIL, ROWS) for z in RING]))
-    for s in LAYERS:
-        write(s, pl.ds(3072, LANES), y[s * 40 : (s + 1) * 40])
-
-
-def pack_tall(even, odd, src, out):
-    def columns(a, b):
-        return stack([src[s, :, a * LANES : b * LANES].astype(F32) for s in LAYERS])
-
-    a, b = dot(even, columns(0, 3)), dot(odd, columns(3, 5))
-    for z in RING:
-        one, rows = [], slice(z * TALL, (z + 1) * TALL)
-        for pair in range(3):
-            u = a[rows, pair * LANES : (pair + 1) * LANES]
-            if pair == 2:
-                one.append(u)
-            else:
-                v = b[rows, pair * LANES : (pair + 1) * LANES]
-                one += [u[:96], u[96:] + v[:8], v[8:]]
-        put(out, z, 0, stack(one))
-
-
-def unpack_tall(even, odd, block, write):
-    for tile in range(5):
-        first = tall_rows(tile, 0) - tile // 3 * 4
-        x = stack([get(block, z, first, first + TALL) for z in RING])
-        y = dot((even, odd)[tile // 3], x)
+        rows = [one[s][z * 50 : (z + 1) * 50] for one in x for s in LAYERS]
+        put(out, z, 0, stack([*rows, jnp.zeros((SIDE, LANES), F32)]))
+
+
+def unpack_tall(block, write):
+    got = [get(block, z, 0, ROWS) for z in RING]
+    for t in range(5):
         for s in LAYERS:
-            write(s, pl.ds(tile * LANES, LANES), y[s * 200 : (s + 1) * 200])
+            row = tall_rows(t, s)
+            write(s, pl.ds(t * LANES, LANES), stack([one[row : row + 50] for one in got]))
 
 
 def each(count, body, start=0):
@@ -195,9 +156,9 @@
 
 
 def step_kernel(*refs):
-    grads, weights, m_in, v_in, mats = (refs[i:j] for i, j in ((0, 3), (3, 6), (6, 9), (9, 12), (12, 16)))
-    new0, new1, mo, vo = refs[16:20]
-    scratch = refs[20:]
+    grads, weights, m_in, v_in = (refs[i : i + 3] for i in (0, 3, 6, 9))
+    new0, new1, mo, vo = refs[12:16]
+    scratch = refs[16:]
     lines, scratch = scratch[:3], scratch[3:]
     own, scratch = [scratch[2 * n : 2 * n + 2] for n in PARTS], scratch[6:]
     packed, scratch = [scratch[2 * n : 2 * n + 2] for n in PARTS], scratch[6:]
@@ -208,7 +169,6 @@
     place = Place((RIGHT, FAR, LEFT))
     at = place.at
     parts = place.parts()
-    mats = [one[...] for one in mats]
 
     def line_copies(srcs, line, slot):
         for n, (src, height) in enumerate(zip(srcs, (40, 40, 200))):
@@ -219,9 +179,9 @@
         for n in PARTS:
             src = lines[n].at[slot]
             if n < 2:
-                pack_wide(*mats[:2], src, outs[n])
+                pack_wide(src, outs[n])
             else:
-                pack_tall(*mats[2:], src, outs[n])
+                pack_tall(src, outs[n])
 
     def distance(u):
         return lax.rem(6 - u + 3 * lax.div(u, 2) - 2 * lax.div(u, 3), 4)
@@ -282,7 +242,7 @@
     for c in line_copies(weights, at(X, ME) * 4 + at(Y, ME), 0):
         c.start()
     for new, old in ((mo, m_in), (vo, v_in)):
-        new[:, 480:ROWS, :] = jnp.zeros((3, TAIL, LANES), F32)
+        new[:, ROWS - TAIL : ROWS, :] = jnp.zeros((3, TAIL, LANES), F32)
         for n in PARTS:
             rows, height, tiles = (tall_rows, 50, 5) if n == 2 else (wide_rows, 10, 25)
             for tile in range(tiles):
@@ -447,7 +407,7 @@
     return jax.ShapeDtypeStruct(dims, dtype)
 
 
-def step(grads, weights, m, v, mats):
+def step(grads, weights, m, v):
     rec = []
     for lead in ((4, 4), (4,), ()):
         a, b = halves(*lead)
@@ -456,7 +416,7 @@
     return pl.pallas_call(
         step_kernel,
         out_shape=[shape(3, HALF[0], LANES), shape(3, HALF[1], LANES)] + [shape(3, ROWS, LANES, dtype=F32)] * 2,
-        in_specs=[ANY] * 6 + [VM] * 10,
+        in_specs=[ANY] * 6 + [VM] * 6,
         out_specs=[VM] * 4,
         scratch_shapes=[
             pltpu.VMEM((2, 2, 40, 3200), BF),
@@ -476,12 +436,12 @@
         ],
         compiler_params=pltpu.CompilerParams(collective_id=0, has_side_effects=True, vmem_limit_bytes=67043328),
         name="step",
-    )(*grads, *weights, *m, *v, *mats)
+    )(*grads, *weights, *m, *v)
 
 
 def gather_kernel(*refs):
-    new, moments, mats, outs, moved = (refs[i:j] for i, j in ((0, 2), (2, 4), (4, 8), (8, 11), (11, 17)))
-    scratch = refs[17:]
+    new, moments, outs, moved = (refs[i:j] for i, j in ((0, 2), (2, 4), (4, 7), (7, 13)))
+    scratch = refs[13:]
     got = [scratch[2 * n : 2 * n + 2] for n in PARTS]
     send, recv, late_send, late_recv = scratch[6:]
     sems = (send, recv)
@@ -576,7 +536,6 @@
                 for s in LAYERS:
                     out[n][:, s, tile * LANES : (tile + 1) * LANES] = one[n, pl.ds(rows(tile, s), height), :]
 
-    mats = [one[...] for one in mats]
 
     def line(p, x, y):
         block = [half.at[x, y] for half in got[p.n]]
@@ -587,9 +546,9 @@
             outs[p.n][layer, rows, columns] = value.astype(BF)
 
         if p.n == 2:
-            unpack_tall(*mats[2:], block, write)
+            unpack_tall(block, write)
         else:
-            unpack_wide(*mats[:2], block, write)
+            unpack_wide(block, write)
 
     def distance(jj):
         return 3 * lax.rem(jj, 2) + lax.div(jj, 2) - 2 * lax.div(jj, 3)
@@ -648,7 +607,7 @@
     each(SIDE, drain)
 
 
-def gather(new, moments, mats):
+def gather(new, moments):
     copies = 90
     wide, tall = (10, 2, 3200), (50, 2, 640)
     outs = [pltpu.VMEM((2, 640, 3200), BF)] * 2 + [pltpu.VMEM((2, 3200, 640), BF)]
@@ -656,7 +615,7 @@
     return pl.pallas_call(
         gather_kernel,
         out_shape=outs,
-        in_specs=[VM] * 8,
+        in_specs=[VM] * 4,
         out_specs=[VM] * MANY,
         scratch_shapes=[
             *halves(*GRID) * 3,
@@ -667,7 +626,7 @@
         ],
         compiler_params=pltpu.CompilerParams(collective_id=1, has_side_effects=True, vmem_limit_bytes=30 * 2**20),
         name="gather",
-    )(*new, *moments, *mats)
+    )(*new, *moments)
 
 
 def finish_kernel(*refs):
@@ -695,9 +654,8 @@
     def run(*arrays):
         terms, weights, m, v = (arrays[i : i + 3] for i in (0, 3, 6, 9))
         swap = lambda arrays: [x.transpose(1, 0, 2) for x in arrays]
-        mats = perms()
-        *new, mo, vo = step([t[0] for t in terms], weights, swap(m), swap(v), [jnp.asarray(a, BF) for a in mats])
-        outs = finish(gather(new, (mo, vo), [jnp.asarray(a.T, BF) for a in mats]))
+        *new, mo, vo = step([t[0] for t in terms], weights, swap(m), swap(v))
+        outs = finish(gather(new, (mo, vo)))
         return (*outs[:3], *swap(outs[3:]))
 
     all_of, cut = P(None, None, None), P(None, "dp", None)

time: 240 us -> 231 us (0.963)
  Pallas kernels: 238 us -> 230 us
    pallas_call x1, Pallas kernels: 112 us -> 104 us  [gather(): pl.pallas_call(gather_kernel, out_shape=outs, in_specs=[VM] * 4, out_spec...]
where the time goes in v3:
time: 231 us
  Pallas kernels  230 us (100%)
    pallas_call x1, Pallas kernels, step(): pl.pallas_call(step_kernel, out_shape=[shape(3, HALF[0], LANES), shape(3,...  117 us
    pallas_call x1, Pallas kernels, gather(): pl.pallas_call(gather_kernel, out_shape=outs, in_specs=[VM] * 4, out_spec...  104 us
    pallas_call x1, Pallas kernels, finish(): pl.pallas_call(finish_kernel, out_shape=[shape(*one.shape, dtype=one.dtyp...  8.79 us

profile of v3, /device:TPU:0, one launch (start us, length us, event | category | flops | bytes accessed | tf_op | source)
XLA Modules:
  0.0 231.0 jit_solution(12997453344105875708)
XLA Ops:
  0.6 117.3 %step.1 = (bf16[3,256,128]{2,1,0:T(8,128)(2,1)}, bf16[3,248,128]{2,1,0:T(8,128)(2,1)}, f32[3,504,128]{2,1,0:T(8,128)}, f32[3,504,128]{2,1,0:T(8,128)}) custom-call(bf16[2,640,3200]{2,1,0:T(8,128)(2,1)} %bitcast.15, bf16[2,640,3200]{2,1,0:T(8,128)(2,1)} %bitcast.16, bf16[2,3200,640]{2,1,0:T(8,128)(2,1)} %bitcast.17, bf16[2,640,3200]{2,1,0:T(8,128)(2,1)} %refs_3_.1, ...), custom_call_target="tpu_custom_call" | custom-call | tf_op jit(solution)/shard_map/step/pallas_call | solution.py:416
  118.0 104.2 %gather.1 = (bf16[2,640,3200]{2,1,0:T(8,128)(2,1)S(1)}, bf16[2,640,3200]{2,1,0:T(8,128)(2,1)S(1)}, bf16[2,3200,640]{2,1,0:T(8,128)(2,1)S(1)}, f32[10,2,3200]{2,1...) custom-call(bf16[3,256,128]{2,1,0:T(8,128)(2,1)} %get-tuple-element., ...), custom_call_target="tpu_custom_call" | custom-call | tf_op jit(solution)/shard_map/gather/pallas_call | solution.py:615
  222.2 8.8 %finish.1 = (bf16[2,640,3200]{2,1,0:T(8,128)(2,1)}, bf16[2,640,3200]{2,1,0:T(8,128)(2,1)}, bf16[2,3200,640]{2,1,0:T(8,128)(2,1)}, f32[10,2,3200]{2,1,0:T(2,128)}...) custom-call(bf16[2,640,3200]{2,1,0:T(8,128)(2,1)S(1)} %get-tuple-ele, ...), custom_call_target="tpu_custom_call" | custom-call | tf_op jit(solution)/shard_map/finish/pallas_call | solution.py:642

commit v4 on v3

--- a/solution.py
+++ b/solution.py
@@ -24,6 +24,8 @@
 ORDERS = ((X, Y, Z), (Y, Z, X), (Z, X, Y))
 PARTS = range(3)
 MANY = 9
+LAG = 2
+ORDER = (ME, LEFT, RIGHT, FAR)
 SIDE, RING, GRID = 4, range(4), (4, 4, 4)
 
 
@@ -109,14 +111,16 @@
 
 
 class Place:
-    def __init__(self, partners):
+    def __init__(self, partners, other_core=False):
         self.rep, dp = lax.axis_index("rep"), lax.axis_index("dp")
         self.here = (lax.div(dp, 16), lax.rem(lax.div(dp, 4), 4), lax.rem(dp, 4))
         barrier = pltpu.get_barrier_semaphore()
         for axis in (X, Y, Z):
             for by in partners:
                 pl.semaphore_signal(barrier, inc=1, device_id=self.device(axis, by), device_id_type=MESH)
-        pl.semaphore_wait(barrier, 3 * len(partners))
+        if other_core:
+            pl.semaphore_signal(barrier, inc=1, device_id=self.other_core(), device_id_type=MESH)
+        pl.semaphore_wait(barrier, 3 * len(partners) + other_core)
         self.count = 0
         self.started = []
 
@@ -126,6 +130,10 @@
     def device(self, axis, by):
         c = [self.at(a, by if a == axis else ME) for a in (X, Y, Z)]
         return (self.rep, c[X] * 16 + c[Y] * 4 + c[Z])
+
+    def other_core(self):
+        c = self.here
+        return (1 - self.rep, c[X] * 16 + c[Y] * 4 + c[Z])
 
     def copy(self, src, dst, axis, by, send, recv):
         return pltpu.make_async_remote_copy(
@@ -163,10 +171,11 @@
     own, scratch = [scratch[2 * n : 2 * n + 2] for n in PARTS], scratch[6:]
     packed, scratch = [scratch[2 * n : 2 * n + 2] for n in PARTS], scratch[6:]
     rec, scratch = [[scratch[18 * n + 6 * f : 18 * n + 6 * f + 6] for f in PARTS] for n in PARTS], scratch[54:]
-    gs, sq, sqr, send, recv, early_send, early_recv, load_sem = scratch
+    gs, sq, sqr, send, recv, early_send, early_recv, load_sem, go = scratch
     sems = (send, recv)
 
-    place = Place((RIGHT, FAR, LEFT))
+    place = Place((RIGHT, FAR, LEFT), True)
+    ahead, behind = place.rep == 1, place.rep == 0
     at = place.at
     parts = place.parts()
 
@@ -202,16 +211,12 @@
     start_line(0)
     start_line(1)
 
-    def first_copies(p, got, kind, piece, block):
-        far_l, far_r, dir_l, dir_r = rec[p.n][FIRST][:4]
-        axis = p.order[FIRST]
-        todo = (
-            ((0, far_l, RIGHT, 0), (1, far_r, LEFT, 1)),
-            ((1, dir_l, RIGHT, 2),),
-            ((0, dir_r, LEFT, 3),),
-        )[kind]
-        for half, to, by, s in todo:
-            place.copy(got[half].at[piece], to.at[block], axis, by, early_send.at[p.n, s], early_recv.at[p.n, s]).start()
+    def early(p, s, src, dst, way):
+        return place.copy(src, dst, p.order[FIRST], way, early_send.at[p.n, s], early_recv.at[p.n, s])
+
+    def to_far(p, piece, block):
+        for half, way in enumerate((RIGHT, LEFT)):
+            early(p, half, packed[p.n][half].at[piece], rec[p.n][FIRST][half].at[block], way).start()
 
     def one_line(t):
         slot = lax.rem(t, 2)
@@ -225,19 +230,35 @@
         def _():
             start_line(t + 2)
 
-        for kind in range(3):
-
-            @pl.when(a == kind)
-            def _():
-                first_copies(parts[0], packed[0], kind, (x, y), y)
-
-            @pl.when(b == kind)
-            def _():
-                first_copies(parts[1], packed[1], kind, (x, y), x)
-
-            first_copies(parts[2], packed[2], kind, (x, y, at(Z, (FAR, RIGHT, LEFT)[kind])), (x, y))
+        @pl.when(a == 0)
+        def _():
+            to_far(parts[0], (x, y), y)
+
+        @pl.when(b == 0)
+        def _():
+            to_far(parts[1], (x, y), x)
+
+        to_far(parts[2], (x, y, at(Z, FAR)), (x, y))
 
     each(16, one_line)
+
+    def whole_pieces(kinds):
+        for p in parts:
+            for s, half, by, way in kinds:
+                piece = place.index(p, at(p.order[FIRST], by), None, None)
+                early(p, s, packed[p.n][half].at[piece], rec[p.n][FIRST][s], way).start()
+
+    NEAR_PIECES = ((2, 1, RIGHT, RIGHT), (3, 0, LEFT, LEFT))
+
+    @pl.when(ahead)
+    def _():
+        whole_pieces(NEAR_PIECES)
+
+    def early_sent():
+        for p in parts:
+            for s in RING:
+                ref = rec[p.n][FIRST][s]
+                early(p, s, ref, ref, LEFT).wait_send()
 
     for c in line_copies(weights, at(X, ME) * 4 + at(Y, ME), 0):
         c.start()
@@ -252,9 +273,14 @@
         c.wait()
     pack(0, own)
 
+    @pl.when(behind)
+    def _():
+        pl.semaphore_wait(go, 1)
+        whole_pieces(NEAR_PIECES)
+
     def early_wait(p, s):
         ref = rec[p.n][FIRST][s]
-        place.copy(ref, ref, p.order[FIRST], LEFT, early_send.at[p.n, s], early_recv.at[p.n, s]).wait_recv()
+        early(p, s, ref, ref, LEFT).wait_recv()
 
     def block(p, ref, j, k):
         return ref.at[(j, k) if p.second else (k, j)]
@@ -309,6 +335,14 @@
 
                 each(SIDE, add)
                 p.com[by].append(place.send(whole(p, got, j), whole(p, to, j), p.order[FIRST], way, sems))
+
+    @pl.when(ahead)
+    def _():
+        early_sent()
+        for c in place.started:
+            c.wait_send()
+        pl.semaphore_signal(go, inc=1, device_id=place.other_core(), device_id_type=MESH)
+
     for p in parts:
         early_wait(p, 2)
         early_wait(p, 3)
@@ -391,12 +425,14 @@
             vo[n, rows, :] = v
             (new0, new1)[half][n] = (w - 0.02 * (m * lax.rsqrt(v + 1e-8) + 0.1 * w)).astype(BF)
 
-    for c in place.started:
+    for c in place.started[24:]:
         c.wait_send()
-    for p in parts:
-        for s in RING:
-            ref = rec[p.n][FIRST][s]
-            place.copy(ref, ref, p.order[FIRST], LEFT, early_send.at[p.n, s], early_recv.at[p.n, s]).wait_send()
+
+    @pl.when(behind)
+    def _():
+        early_sent()
+        for c in place.started[:24]:
+            c.wait_send()
 
 
 def halves(*lead, dtype=BF):
@@ -433,6 +469,7 @@
             pltpu.SemaphoreType.DMA((3, 4)),
             pltpu.SemaphoreType.DMA((3, 4)),
             pltpu.SemaphoreType.DMA((2, 3)),
+            pltpu.SemaphoreType.REGULAR,
         ],
         compiler_params=pltpu.CompilerParams(collective_id=0, has_side_effects=True, vmem_limit_bytes=67043328),
         name="step",
@@ -484,15 +521,21 @@
     def along(p):
         return p.order[THIRD if p.n == 1 else SECOND]
 
-    def last_spread(p, jj, by):
-        index = chunk(p, p.me[FIRST], at(along(p), by))
+    def last_spread(p, j, k):
+        jj = ORDER.index(k if p.n == 1 else j)
+        mine = j == ME and k == ME
+        index = (p.me[FIRST], at(p.order[SECOND], j), at(p.order[THIRD], k))
         for e, (h, way) in enumerate(((0, RIGHT), (1, LEFT), (1, RIGHT), (0, LEFT))):
-            late(p, jj, e, h, index, way).start()
+            to = ref_of(p, h, *index)
+            sems = late_send.at[p.n, jj, e], late_recv.at[p.n, jj, e]
+            place.copy(new[h].at[p.n] if mine else to, to, p.order[FIRST], way, *sems).start()
 
     for p in parts:
         p.s3 = spread(p, p.order[THIRD], *p.me, mine=True)
     for p in parts:
         p.s2, p.f2 = [spread(p, p.order[SECOND], *p.me, mine=True)], []
+    for p in parts:
+        last_spread(p, ME, ME)
     for p in parts:
         for h in LAYERS:
             ref_of(p, h, *p.me)[...] = new[h][p.n]
@@ -504,30 +547,25 @@
         for k in (p.left[THIRD], p.right[THIRD]):
             p.s2.append(spread(p, p.order[SECOND], *p.me[:THIRD], k))
     for p in parts:
+        last_spread(p, ME, LEFT)
+        last_spread(p, ME, RIGHT)
+    for p in parts:
         arrived(*p.f3)
         p.s2.append(spread(p, p.order[SECOND], *p.me[:THIRD], p.far[THIRD]))
-        if p.n != 1:
-            last_spread(p, 0, ME)
-    for step, by in enumerate((ME, LEFT, RIGHT, FAR)):
-        for p in parts:
-            i, k = p.me[FIRST], p.steps[step][THIRD]
-            p.f2.append(forward(p, p.order[SECOND], p.s2[step], (i, p.left[SECOND], k), (i, p.right[SECOND], k)))
-        p = parts[1]
-        if step:
-            arrived(*p.s2[step - 1][2:], *p.f2[step - 1])
-            last_spread(p, step - 1, (ME, LEFT, RIGHT)[step - 1])
-    for p in parts:
-        if p.n == 1:
-            arrived(*p.s2[3][2:], *p.f2[3])
-            last_spread(p, 3, FAR)
-        else:
-            for copies in p.s2:
-                arrived(*copies[2:])
-            last_spread(p, 1, LEFT)
-            last_spread(p, 2, RIGHT)
-            for copies in p.f2:
-                arrived(*copies)
-            last_spread(p, 3, FAR)
+        last_spread(p, ME, FAR)
+    for step, by in enumerate((*ORDER, None)):
+        for p in parts:
+            if by is not None:
+                i, k = p.me[FIRST], p.steps[step][THIRD]
+                p.f2.append(forward(p, p.order[SECOND], p.s2[step], (i, p.left[SECOND], k), (i, p.right[SECOND], k)))
+        for p in parts:
+            if by is not None:
+                arrived(*p.s2[step][2:])
+                last_spread(p, LEFT, by)
+                last_spread(p, RIGHT, by)
+            if step:
+                arrived(*p.f2[step - 1])
+                last_spread(p, FAR, ORDER[step - 1])
 
     for out, one in zip((moved[:3], moved[3:]), moments):
         for n in PARTS:
@@ -569,9 +607,9 @@
                 late(p, jj, 2, 1, left, LEFT).wait_recv()
                 late(p, jj, 3, 0, right, LEFT).wait_recv()
 
-        before = jj - 1
-
-        @pl.when(jj > 0)
+        before = jj - LAG
+
+        @pl.when(jj >= LAG)
         def _():
             for p in parts:
                 far = chunk(p, p.far[FIRST], at(along(p), distance(before)))
@@ -579,7 +617,7 @@
                 late(p, before, 5, 1, far, LEFT).wait_recv()
 
         def one(i):
-            which = jj - lax.div(i, 3)
+            which = jj - LAG * lax.div(i, 3)
 
             @pl.when((which >= 0) & (which < 4))
             def _():
@@ -587,13 +625,13 @@
                 line(parts[0], at(X, distance(i)), at(Y, value))
                 line(parts[1], at(X, value), at(Y, distance(i)))
 
-            @pl.when(jj > 0)
+            @pl.when(jj >= LAG)
             def _():
                 line(parts[2], at(X, distance(before)), i)
 
         each(SIDE, one)
 
-    each(5, last)
+    each(SIDE + LAG, last)
 
     for c in place.started:
         c.wait_send()

time: 231 us -> 203 us (0.88)
  Pallas kernels: 230 us -> 202 us
    pallas_call x1, Pallas kernels: 104 us -> 71.6 us  [gather(): pl.pallas_call(gather_kernel, out_shape=outs, in_specs=[VM] * 4, out_spec...]
    pallas_call x1, Pallas kernels: 117 us -> 122 us  [step(): pl.pallas_call(step_kernel, out_shape=[shape(3, HALF[0], LANES), shape(3,...]
where the time goes in v4:
time: 203 us
  Pallas kernels  202 us (100%)
    pallas_call x1, Pallas kernels, step(): pl.pallas_call(step_kernel, out_shape=[shape(3, HALF[0], LANES), shape(3,...  122 us
    pallas_call x1, Pallas kernels, gather(): pl.pallas_call(gather_kernel, out_shape=outs, in_specs=[VM] * 4, out_spec...  71.6 us
    pallas_call x1, Pallas kernels, finish(): pl.pallas_call(finish_kernel, out_shape=[shape(*one.shape, dtype=one.dtyp...  8.79 us

profile of v4, /device:TPU:0, one launch (start us, length us, event | category | flops | bytes accessed | tf_op | source)
XLA Modules:
  0.0 202.7 jit_solution(7485656515791470537)
XLA Ops:
  0.6 121.6 %step.1 = (bf16[3,256,128]{2,1,0:T(8,128)(2,1)}, bf16[3,248,128]{2,1,0:T(8,128)(2,1)}, f32[3,504,128]{2,1,0:T(8,128)}, f32[3,504,128]{2,1,0:T(8,128)}) custom-call(bf16[2,640,3200]{2,1,0:T(8,128)(2,1)} %bitcast.15, bf16[2,640,3200]{2,1,0:T(8,128)(2,1)} %bitcast.16, bf16[2,3200,640]{2,1,0:T(8,128)(2,1)} %bitcast.17, bf16[2,640,3200]{2,1,0:T(8,128)(2,1)} %refs_3_.1, ...), custom_call_target="tpu_custom_call" | custom-call | tf_op jit(solution)/shard_map/step/pallas_call | solution.py:452
  122.3 71.6 %gather.1 = (bf16[2,640,3200]{2,1,0:T(8,128)(2,1)S(1)}, bf16[2,640,3200]{2,1,0:T(8,128)(2,1)S(1)}, bf16[2,3200,640]{2,1,0:T(8,128)(2,1)S(1)}, f32[10,2,3200]{2,1...) custom-call(bf16[3,256,128]{2,1,0:T(8,128)(2,1)} %get-tuple-element., ...), custom_call_target="tpu_custom_call" | custom-call | tf_op jit(solution)/shard_map/gather/pallas_call | solution.py:653
  193.9 8.8 %finish.1 = (bf16[2,640,3200]{2,1,0:T(8,128)(2,1)}, bf16[2,640,3200]{2,1,0:T(8,128)(2,1)}, bf16[2,3200,640]{2,1,0:T(8,128)(2,1)}, f32[10,2,3200]{2,1,0:T(2,128)}...) custom-call(bf16[2,640,3200]{2,1,0:T(8,128)(2,1)S(1)} %get-tuple-ele, ...), custom_call_target="tpu_custom_call" | custom-call | tf_op jit(solution)/shard_map/finish/pallas_call | solution.py:680

commit v5 on v4

--- a/solution.py
+++ b/solution.py
@@ -120,7 +120,7 @@
                 pl.semaphore_signal(barrier, inc=1, device_id=self.device(axis, by), device_id_type=MESH)
         if other_core:
             pl.semaphore_signal(barrier, inc=1, device_id=self.other_core(), device_id_type=MESH)
-        pl.semaphore_wait(barrier, 3 * len(partners) + other_core)
+        self.barrier, self.greeted = barrier, 3 * len(partners) + other_core
         self.count = 0
         self.started = []
 
@@ -130,6 +130,9 @@
     def device(self, axis, by):
         c = [self.at(a, by if a == axis else ME) for a in (X, Y, Z)]
         return (self.rep, c[X] * 16 + c[Y] * 4 + c[Z])
+
+    def wait(self):
+        pl.semaphore_wait(self.barrier, self.greeted)
 
     def other_core(self):
         c = self.here
@@ -218,7 +221,7 @@
         for half, way in enumerate((RIGHT, LEFT)):
             early(p, half, packed[p.n][half].at[piece], rec[p.n][FIRST][half].at[block], way).start()
 
-    def one_line(t):
+    def one_line(t, first=False):
         slot = lax.rem(t, 2)
         a, b = where(t)
         x, y = line_of(t)
@@ -230,6 +233,9 @@
         def _():
             start_line(t + 2)
 
+        if first:
+            place.wait()
+
         @pl.when(a == 0)
         def _():
             to_far(parts[0], (x, y), y)
@@ -240,7 +246,8 @@
 
         to_far(parts[2], (x, y, at(Z, FAR)), (x, y))
 
-    each(16, one_line)
+    one_line(0, True)
+    each(16, one_line, start=1)
 
     def whole_pieces(kinds):
         for p in parts:
@@ -484,6 +491,7 @@
     sems = (send, recv)
 
     place = Place((RIGHT, LEFT))
+    place.wait()
     at = place.at
     parts = place.parts()
     for p in parts:

time: 203 us -> 201 us (level)
  no operation moved by 1% of the time
where the time goes in v5:
time: 201 us
  Pallas kernels  200 us (100%)
    pallas_call x1, Pallas kernels, step(): pl.pallas_call(step_kernel, out_shape=[shape(3, HALF[0], LANES), shape(3,...  120 us
    pallas_call x1, Pallas kernels, gather(): pl.pallas_call(gather_kernel, out_shape=outs, in_specs=[VM] * 4, out_spec...  71.6 us
    pallas_call x1, Pallas kernels, finish(): pl.pallas_call(finish_kernel, out_shape=[shape(*one.shape, dtype=one.dtyp...  8.79 us

profile of v5, /device:TPU:0, one launch (start us, length us, event | category | flops | bytes accessed | tf_op | source)
XLA Modules:
  0.0 200.9 jit_solution(6896237706322568575)
XLA Ops:
  0.6 119.8 %step.1 = (bf16[3,256,128]{2,1,0:T(8,128)(2,1)}, bf16[3,248,128]{2,1,0:T(8,128)(2,1)}, f32[3,504,128]{2,1,0:T(8,128)}, f32[3,504,128]{2,1,0:T(8,128)}) custom-call(bf16[2,640,3200]{2,1,0:T(8,128)(2,1)} %bitcast.15, bf16[2,640,3200]{2,1,0:T(8,128)(2,1)} %bitcast.16, bf16[2,3200,640]{2,1,0:T(8,128)(2,1)} %bitcast.17, bf16[2,640,3200]{2,1,0:T(8,128)(2,1)} %refs_3_.1, ...), custom_call_target="tpu_custom_call" | custom-call | tf_op jit(solution)/shard_map/step/pallas_call | solution.py:459
  120.5 71.6 %gather.1 = (bf16[2,640,3200]{2,1,0:T(8,128)(2,1)S(1)}, bf16[2,640,3200]{2,1,0:T(8,128)(2,1)S(1)}, bf16[2,3200,640]{2,1,0:T(8,128)(2,1)S(1)}, f32[10,2,3200]{2,1...) custom-call(bf16[3,256,128]{2,1,0:T(8,128)(2,1)} %get-tuple-element., ...), custom_call_target="tpu_custom_call" | custom-call | tf_op jit(solution)/shard_map/gather/pallas_call | solution.py:661
  192.1 8.8 %finish.1 = (bf16[2,640,3200]{2,1,0:T(8,128)(2,1)}, bf16[2,640,3200]{2,1,0:T(8,128)(2,1)}, bf16[2,3200,640]{2,1,0:T(8,128)(2,1)}, f32[10,2,3200]{2,1,0:T(2,128)}...) custom-call(bf16[2,640,3200]{2,1,0:T(8,128)(2,1)S(1)} %get-tuple-ele, ...), custom_call_target="tpu_custom_call" | custom-call | tf_op jit(solution)/shard_map/finish/pallas_call | solution.py:688

commit v6 on v5

--- a/solution.py
+++ b/solution.py
@@ -24,7 +24,7 @@
 ORDERS = ((X, Y, Z), (Y, Z, X), (Z, X, Y))
 PARTS = range(3)
 MANY = 9
-LAG = 2
+LAG = 3
 ORDER = (ME, LEFT, RIGHT, FAR)
 SIDE, RING, GRID = 4, range(4), (4, 4, 4)
 
@@ -491,7 +491,6 @@
     sems = (send, recv)
 
     place = Place((RIGHT, LEFT))
-    place.wait()
     at = place.at
     parts = place.parts()
     for p in parts:
@@ -539,14 +538,16 @@
             place.copy(new[h].at[p.n] if mine else to, to, p.order[FIRST], way, *sems).start()
 
     for p in parts:
-        p.s3 = spread(p, p.order[THIRD], *p.me, mine=True)
-    for p in parts:
-        p.s2, p.f2 = [spread(p, p.order[SECOND], *p.me, mine=True)], []
-    for p in parts:
-        last_spread(p, ME, ME)
-    for p in parts:
         for h in LAYERS:
             ref_of(p, h, *p.me)[...] = new[h][p.n]
+    place.wait()
+
+    for p in parts:
+        p.s3 = spread(p, p.order[THIRD], *p.me, mine=True)
+    for p in parts:
+        p.s2, p.f2 = [spread(p, p.order[SECOND], *p.me, mine=True)], []
+    for p in parts:
+        last_spread(p, ME, ME)
     for p in parts:
         i, j, k = p.me
         p.f3 = forward(p, p.order[THIRD], p.s3, (i, j, p.left[THIRD]), (i, j, p.right[THIRD]))

time: 201 us -> 201 us (level)
  no operation moved by 1% of the time
where the time goes in v6:
time: 201 us
  Pallas kernels  200 us (100%)
    pallas_call x1, Pallas kernels, step(): pl.pallas_call(step_kernel, out_shape=[shape(3, HALF[0], LANES), shape(3,...  120 us
    pallas_call x1, Pallas kernels, gather(): pl.pallas_call(gather_kernel, out_shape=outs, in_specs=[VM] * 4, out_spec...  71.6 us
    pallas_call x1, Pallas kernels, finish(): pl.pallas_call(finish_kernel, out_shape=[shape(*one.shape, dtype=one.dtyp...  8.79 us

profile of v6, /device:TPU:0, one launch (start us, length us, event | category | flops | bytes accessed | tf_op | source)
XLA Modules:
  0.0 200.9 jit_solution(14008270345784099515)
XLA Ops:
  0.6 119.8 %step.1 = (bf16[3,256,128]{2,1,0:T(8,128)(2,1)}, bf16[3,248,128]{2,1,0:T(8,128)(2,1)}, f32[3,504,128]{2,1,0:T(8,128)}, f32[3,504,128]{2,1,0:T(8,128)}) custom-call(bf16[2,640,3200]{2,1,0:T(8,128)(2,1)} %bitcast.15, bf16[2,640,3200]{2,1,0:T(8,128)(2,1)} %bitcast.16, bf16[2,3200,640]{2,1,0:T(8,128)(2,1)} %bitcast.17, bf16[2,640,3200]{2,1,0:T(8,128)(2,1)} %refs_3_.1, ...), custom_call_target="tpu_custom_call" | custom-call | tf_op jit(solution)/shard_map/step/pallas_call | solution.py:459
  120.5 71.6 %gather.1 = (bf16[2,640,3200]{2,1,0:T(8,128)(2,1)S(1)}, bf16[2,640,3200]{2,1,0:T(8,128)(2,1)S(1)}, bf16[2,3200,640]{2,1,0:T(8,128)(2,1)S(1)}, f32[10,2,3200]{2,1...) custom-call(bf16[3,256,128]{2,1,0:T(8,128)(2,1)} %get-tuple-element., ...), custom_call_target="tpu_custom_call" | custom-call | tf_op jit(solution)/shard_map/gather/pallas_call | solution.py:662
  192.1 8.8 %finish.1 = (bf16[2,640,3200]{2,1,0:T(8,128)(2,1)}, bf16[2,640,3200]{2,1,0:T(8,128)(2,1)}, bf16[2,3200,640]{2,1,0:T(8,128)(2,1)}, f32[10,2,3200]{2,1,0:T(2,128)}...) custom-call(bf16[2,640,3200]{2,1,0:T(8,128)(2,1)S(1)} %get-tuple-ele, ...), custom_call_target="tpu_custom_call" | custom-call | tf_op jit(solution)/shard_map/finish/pallas_call | solution.py:689
